TPU v7x, 256 devices: a whole 4x4x8 slice. The times are simulated.
256 devices in a mesh: dp: 64 (over z, x, core), outer: 4 (over y).
Axes of the slice: x: 4, y: 4, z: 8, core: 2. Of those that a mesh axis runs over, the one named last changes fastest.
Arguments:
- partials: bfloat16 [4, 64, 2, 128, 8192], P('outer', 'dp'), may hold values from -3500 to 3500, as said below
- master: float32 [2, 128, 8192], P(None, 'dp'), may hold values from -6 to 6
- m_codes: bfloat16 [2, 128, 8192], P(None, 'dp'), may hold values from -1 to 1
- v_codes: bfloat16 [2, 128, 8192], P(None, 'dp'), may hold values from 0.049804688 to 1
- m_scales: float32 [2, 128, 4], P(None, 'dp'), may hold values from 0.0001 to 0.001
- v_scales: float32 [2, 128, 4], P(None, 'dp'), may hold values from 1e-08 to 1e-07
Outputs:
- new_master: float32 [2, 128, 8192], P(None, 'dp')
- new_m_codes: bfloat16 [2, 128, 8192], P(None, 'dp')
- new_v_codes: bfloat16 [2, 128, 8192], P(None, 'dp')
- new_m_scales: float32 [2, 128, 4], P(None, 'dp')
- new_v_scales: float32 [2, 128, 4], P(None, 'dp')
- weights: bfloat16 [2, 128, 8192], replicated
Inputs may be any that keep to these rules, and one draw needn't show every extreme that they name: Gradient partials of real values; entries vary from row to row and column to column.
All inputs are finite; a program needn't handle non-finite values. Where the computation divides by a largest or mean magnitude, that divisor is 1e-20 or more.
Results may differ from a plain program's by a relative error of at most 0.0004.
Values may be sent and summed in bfloat16 or wider, within the bound.
A program may use at most 64 MiB of HBM per device.

v0:
```python
import functools

import jax
import jax.numpy as jnp
from jax import lax
from jax.sharding import Mesh
from jax.sharding import PartitionSpec as P

BLOCK = 2048
STEP = 10
DP = ("dp_0", "dp_1", "dp_2")
DP_OUTER = ("dp_0", "dp_1", "dp_2", "outer")


def cut_along(x, dim, count):
    lengths = x.shape
    pieces = x.reshape(*lengths[:dim], count, lengths[dim] // count, *lengths[dim + 1 :])
    return jnp.moveaxis(pieces, dim, 0)


def sum_at_owner(x, axis, dim):
    pieces = cut_along(x, dim, lax.axis_size(axis))
    arrived = lax.all_to_all(pieces, axis, split_axis=0, concat_axis=0, tiled=True)
    return arrived.sum(axis=0)


def over_axes(x, axes):
    return functools.reduce(lax.psum, axes, x)


def sent_together(arrays, axis, dim, along):
    widths = [a.shape[along] for a in arrays]
    both = jnp.concatenate(arrays, axis=along)
    result = lax.all_gather(both, axis, axis=dim, tiled=True)
    return tuple(jnp.split(result, [sum(widths[:k]) for k in range(1, len(widths))], axis=along))


def in_order(pieces, dim):
    lengths = list(pieces.shape[1:])
    lengths[dim] *= pieces.shape[0]
    return jnp.moveaxis(pieces, 0, dim).reshape(lengths)


def gather_in_order(x, axes, order):
    pieces = x[None]
    for k in order:
        pieces = lax.all_gather(pieces, axes[k], axis=0, tiled=True)
    block = [lax.axis_size(axes[k]) for k in reversed(order)]
    pieces = pieces.reshape(*block, *x.shape)
    turned = sorted(range(len(order)), key=lambda place: order[len(order) - 1 - place])
    return pieces.transpose(*turned, *range(len(order), pieces.ndim)).reshape(-1, *x.shape)


def whole_of(x, axes, order, dim):
    return in_order(gather_in_order(x, axes, order), dim)


def adam_blocks(gradient, master, m_codes, v_codes, m_scales, v_scales, clip_factor):
    count = gradient.shape[0]
    rows = gradient.shape[1]
    blocks = gradient.shape[2] // BLOCK
    shape_four = (count, rows, blocks, BLOCK)
    moment = m_codes.astype(jnp.float32).reshape(shape_four) * m_scales[..., None]
    second = v_codes.astype(jnp.float32).reshape(shape_four) * v_scales[..., None]
    scaled = clip_factor * gradient.reshape(shape_four)
    moment = 0.9 * moment + 0.1 * scaled
    second = 0.95 * second + 0.05 * scaled * scaled
    update = moment / (1.0 - 0.9**STEP) / (jnp.sqrt(second / (1.0 - 0.95**STEP)) + 1e-08)
    fresh = master - 0.01 * update.reshape(master.shape)
    m_top = jnp.max(jnp.abs(moment), axis=3) + 1e-20
    v_top = jnp.max(jnp.abs(second), axis=3) + 1e-20
    m_next = (moment / m_top[..., None]).astype(jnp.bfloat16).reshape(master.shape)
    v_next = (second / v_top[..., None]).astype(jnp.bfloat16).reshape(master.shape)
    return (fresh, m_next, v_next, m_top, v_top, fresh.astype(jnp.bfloat16))


def body(partials, master, m_codes, v_codes, m_scales, v_scales):
    own_terms = partials[0, 0]
    received = lax.all_to_all(own_terms[None], "outer", split_axis=3, concat_axis=0, tiled=True)
    column_part = jnp.sum(received.astype(jnp.float32), axis=0)
    gradient = sum_at_owner(column_part, DP, 1)
    total = over_axes(jnp.sum(gradient * gradient), DP_OUTER)
    clip_factor = 1.0 / jnp.maximum(jnp.sqrt(total), 1.0)
    quarter = gradient.shape[2]
    offset = lax.axis_index("outer") * quarter
    scale_count = quarter // BLOCK
    scale_offset = lax.axis_index("outer") * scale_count
    results = adam_blocks(
        gradient,
        lax.dynamic_slice_in_dim(master, offset, quarter, 2),
        lax.dynamic_slice_in_dim(m_codes, offset, quarter, 2),
        lax.dynamic_slice_in_dim(v_codes, offset, quarter, 2),
        lax.dynamic_slice_in_dim(m_scales, scale_offset, scale_count, 2),
        lax.dynamic_slice_in_dim(v_scales, scale_offset, scale_count, 2),
        clip_factor,
    )
    fresh, m_next, v_next, m_top, v_top, rounded = results
    fresh, m_top, v_top = (
        lax.all_gather(fresh, "outer", axis=2, tiled=True),
        *sent_together((m_top, v_top), "outer", 2, 0),
    )
    m_next, v_next, rounded = sent_together((m_next, v_next, rounded), "outer", 2, 0)
    weights = whole_of(rounded, DP, (1, 0, 2), 1)
    return (fresh, m_next, v_next, m_top, v_top, weights)


def solution(mesh):
    finer = Mesh(
        mesh.devices.reshape(8, 4, 2, mesh.shape["outer"]), ("dp_0", "dp_1", "dp_2", "outer")
    )
    placed = (
        P("outer", DP, None, None, None),
        P(None, DP, None),
        P(None, DP, None),
        P(None, DP, None),
        P(None, DP, None),
        P(None, DP, None),
    )
    return jax.shard_map(
        body,
        mesh=finer,
        in_specs=placed,
        out_specs=(
            P(None, DP, None),
            P(None, DP, None),
            P(None, DP, None),
            P(None, DP, None),
            P(None, DP, None),
            P(),
        ),
        check_vma=False,
    )
```

profile of v0, /device:TPU:1, one launch (start us, length us, event | category | flops | bytes accessed | tf_op | source)
XLA Modules:
  0.0 301.3 jit_solution(3375123823743726198)
XLA Ops:
  7.2 11.2 %copy.36 = bf16[1,1,2,128,8192]{3,2,4,1,0:T(2,128)(2,1)} copy(bf16[1,1,2,128,8192]{4,3,2,1,0:T(8,128)(2,1)} %param.6) | data formatting | bytes 8388608 | tf_op args[0]
  18.3 51.9 %all_to_all.14 = bf16[1,2,128,8192]{2,1,0,3:T(2,128)(2,1)S(1)} all-to-all(bf16[1,2,128,8192]{2,1,0,3:T(2,128)(2,1)} %bitcast.21), channel_id=1, replica_groups=mesh['dp_0'=8,'dp_1'=4,'dp_2'=2,'outer'=4] {'outer'}, dimensions={3} | all-to-all | bytes 8388608 | tf_op jit(solution)/shard_map/all_to_all | solution.py:79
  70.3 5.1 %convert_reduce_fusion = f32[2,128,2048]{1,0,2:T(2,128)S(1)} fusion(bf16[2,128,4,2048]{1,0,3,2:T(2,128)(2,1)S(1)} %bitcast.18), kind=kLoop, calls=%fused_computation | loop fusion | flops 3670016 | bytes 6291456 | tf_op jit(solution)/shard_map/reduce_sum | solution.py:80
  75.4 3.5 %copy.37 = f32[2,128,2048]{2,0,1:T(2,128)} copy(f32[2,128,2048]{1,0,2:T(2,128)S(1)} %convert_reduce_fusion) | data formatting | bytes 4194304 | tf_op jit(solution)/shard_map/reduce_sum | solution.py:80
  78.9 4.9 %copy.38 = f32[64,2,2,2048]{3,2,1,0:T(2,128)} copy(f32[64,2,2,2048]{3,1,2,0:T(2,128)} %bitcast.22) | data formatting | bytes 4194304 | tf_op jit(solution)/shard_map/transpose | solution.py:18
  83.8 14.3 %all-to-all-start.1 = ((f32[64,2,2,2048]{3,2,1,0:T(2,128)}), f32[64,2,2,2048]{3,2,1,0:T(2,128)S(1)}, u32[]{:S(2)}, u32[]{:S(2)}) async-start(f32[64,2,2,2048]{3,2,1,0:T(2,128)} %copy.38), calls=%async_computation.1 | async-start | bytes 4194304 | tf_op jit(solution)/shard_map/all_to_all | solution.py:23
  98.3 49.5 %all-to-all-done.1 = f32[64,2,2,2048]{3,2,1,0:T(2,128)S(1)} async-done(((f32[64,2,2,2048]{3,2,1,0:T(2,128)}), f32[64,2,2,2048]{3,2,1,0:T(2,128)S(1)}, u32[]{:S(2)}, u32[]{:S(2)}) %all-to-all-start.1) | async-done | bytes 2097184 | tf_op jit(solution)/shard_map/all_to_all | solution.py:23
  147.8 0.8 reduce_sum.28
  149.3 13.4 %psum.28 = f32[]{:T(128)} all-reduce(f32[]{:T(128)} %multiply_reduce_fusion), channel_id=1, replica_groups=mesh['dp_0'=8,'dp_1'=4,'dp_2'=2,'outer'=4] {'dp_0'}, use_global_device_ids=true, to_apply=%region_3.0 | all-reduce | flops 1 | bytes 8 | tf_op jit(solution)/shard_map/psum | solution.py:28
  162.7 8.3 %psum.29 = f32[]{:T(128)} all-reduce(f32[]{:T(128)} %psum.28), channel_id=1, replica_groups=mesh['dp_0'=8,'dp_1'=4,'dp_2'=2,'outer'=4] {'dp_1'}, use_global_device_ids=true, to_apply=%region_4.0 | all-reduce | flops 1 | bytes 8 | tf_op jit(solution)/shard_map/psum | solution.py:28
  170.9 9.6 %psum.30 = f32[]{:T(128)} all-reduce(f32[]{:T(128)} %psum.29), channel_id=1, replica_groups=mesh['dp_0'=8,'dp_1'=4,'dp_2'=2,'outer'=4] {'dp_2'}, use_global_device_ids=true, to_apply=%region_5.0 | all-reduce | flops 1 | bytes 8 | tf_op jit(solution)/shard_map/psum | solution.py:28
  180.5 7.5 %psum.31 = f32[]{:T(128)} all-reduce(f32[]{:T(128)} %psum.30), channel_id=1, replica_groups=mesh['dp_0'=8,'dp_1'=4,'dp_2'=2,'outer'=4] {'outer'}, use_global_device_ids=true, to_apply=%region_6.0 | all-reduce | flops 1 | bytes 8 | tf_op jit(solution)/shard_map/psum | solution.py:28
  188.7 1.0 abs_reduce_fusion.1
  189.7 0.9 fusion.4
  190.6 9.4 %all_gather.19 = bf16[6,2,8192]{2,1,0:T(2,128)(2,1)S(1)} all-gather(bf16[6,2,2048]{2,1,0:T(2,128)(2,1)S(1)} %pad_maximum_fusion), channel_id=1, replica_groups=mesh['dp_0'=8,'dp_1'=4,'dp_2'=2,'outer'=4] {'outer'}, dimensions={2}, use_global_device_ids=true | all-gather | bytes 245760 | tf_op jit(solution)/shard_map/all_gather | solution.py:34
  200.1 0.8 fusion.5
  200.8 10.6 %all-gather = bf16[8,2,8192]{2,1,0:T(2,128)(2,1)} all-gather(bf16[2,2,8192]{2,1,0:T(2,128)(2,1)S(1)} %get-tuple-element.48), channel_id=2, replica_groups=mesh['dp_0'=8,'dp_1'=4,'dp_2'=2,'outer'=4] {'dp_1'}, dimensions={0}, use_global_device_ids=true | all-gather | bytes 327680 | tf_op jit(solution)/shard_map/all_gather | solution.py:47
  211.5 38.7 %all-gather.4.cloned.1.call-done = bf16[32,2,2,8192]{3,2,1,0:T(2,128)(2,1)} async-done(((bf16[4,2,2,8192]{3,2,1,0:T(2,128)(2,1)}), bf16[32,2,2,8192]{3,2,1,0:T(2,128)(2,1)}) %all-gather.4.cloned.1.call-update) | async-done | bytes 2097168 | tf_op jit(solution)/shard_map/all_gather | solution.py:47
  250.3 7.7 %all_gather.20 = f32[4,2,4]{0,1,2:T(2,128)S(1)} all-gather(f32[4,2,1]{0,1,2:T(2,128)S(1)} %copy.39), channel_id=1, replica_groups=mesh['dp_0'=8,'dp_1'=4,'dp_2'=2,'outer'=4] {'outer'}, dimensions={2}, use_global_device_ids=true | all-gather | bytes 160 | tf_op jit(solution)/shard_map/all_gather | solution.py:34
  258.0 9.3 %all_gather.18 = f32[2,2,8192]{2,1,0:T(2,128)S(1)} all-gather(f32[2,2,2048]{2,1,0:T(2,128)S(1)} %get-tuple-element.47), channel_id=1, replica_groups=mesh['dp_0'=8,'dp_1'=4,'dp_2'=2,'outer'=4] {'outer'}, dimensions={2}, use_global_device_ids=true | all-gather | bytes 163840 | tf_op jit(solution)/shard_map/all_gather | solution.py:99
  268.7 5.8 %all-gather.6.cloned.1.call-done = bf16[64,2,2,8192]{3,2,1,0:T(2,128)(2,1)} async-done(((bf16[32,2,2,8192]{3,2,1,0:T(2,128)(2,1)}), bf16[64,2,2,8192]{3,2,1,0:T(2,128)(2,1)}) %all-gather.6.cloned.1.call-update) | async-done | bytes 4194320 | tf_op jit(solution)/shard_map/all_gather | solution.py:47
  274.5 6.1 %copy.40 = bf16[2,8,4,2,2,8192]{5,4,3,0,2,1:T(2,128)(2,1)S(1)} copy(bf16[2,8,4,2,2,8192]{5,4,3,2,1,0:T(2,128)(2,1)} %bitcast.23) | data formatting | bytes 8388608 | tf_op jit(solution)/shard_map/reshape | solution.py:49
  280.6 6.3 %copy.41 = bf16[2,64,2,8192]{3,0,2,1:T(2,128)(2,1)} copy(bf16[2,64,2,8192]{3,2,0,1:T(2,128)(2,1)S(1)} %bitcast.19) | data formatting | bytes 8388608 | tf_op jit(solution)/shard_map/transpose | solution.py:41
  286.9 6.9 %copy.44 = bf16[2,128,8192]{2,1,0:T(8,128)(2,1)} copy(bf16[2,128,8192]{2,0,1:T(2,128)(2,1)} %bitcast.20) | data formatting | bytes 8388608
  (19 shorter events, 3.2 us)
Async XLA Ops:
  78.9 19.2 %copy-start = (f32[2,2,4]{2,1,0:T(2,128)S(1)}, f32[2,2,4]{2,1,0:T(2,128)}, u32[]{:S(2)}) copy-start(f32[2,2,4]{2,1,0:T(2,128)} %param.11) | copy-start | bytes 196
  78.9 19.2 %copy-start.1 = (f32[2,2,4]{2,1,0:T(2,128)S(1)}, f32[2,2,4]{2,1,0:T(2,128)}, u32[]{:S(2)}) copy-start(f32[2,2,4]{2,1,0:T(2,128)} %param.10) | copy-start | bytes 196
  83.8 64.0 %all-to-all-start.1 = ((f32[64,2,2,2048]{3,2,1,0:T(2,128)}), f32[64,2,2,2048]{3,2,1,0:T(2,128)S(1)}, u32[]{:S(2)}, u32[]{:S(2)}) async-start(f32[64,2,2,2048]{3,2,1,0:T(2,128)} %copy.38), calls=%async_computation.1 | async-start | bytes 4194304 | tf_op jit(solution)/shard_map/all_to_all | solution.py:23
  98.1 152.1 %all-gather.4.cloned.1.call-start = ((), (), s32[]{:S(2)}) async-start(), calls=%async_computation.2 | async-start | bytes 2359296 | tf_op jit(solution)/shard_map/all_gather | solution.py:47
  211.5 63.0 %all-gather.6.cloned.1.call-start = ((), (), s32[]{:S(2)}) async-start(), calls=%async_computation.3 | async-start | bytes 6291456 | tf_op jit(solution)/shard_map/all_gather | solution.py:47
Sparse Core Ops, SparseCore 0:
  211.6 38.5 all-gather.3
  252.0 22.4 all-gather.5
where the time goes:
time: 305 us; the launch traced here: 301 us
  blocking collectives  128 us (42%)
  waiting for transfers between devices  94 us (31%)
  local copies, waits for them, and re-layouts  42 us (14%)
  between operations  14.8 us (5%)
  starting transfers between devices  14.4 us (5%)
  other arithmetic  8.43 us (3%)
    all_to_all x1, blocking collectives, body(): lax.all_to_all(own_terms[None], 'outer', split_axis=3, concat_axis=0, til...  51.9 us
    all_to_all x1, waiting for transfers between devices, sum_at_owner(): lax.all_to_all(pieces, axis, split_axis=0, concat_axis=0, tiled=True)  49.5 us
    all_gather x2, waiting for transfers between devices, gather_in_order(): pieces = lax.all_gather(pieces, axes[k], axis=0, tiled=True)  44.5 us
    psum x4, blocking collectives, over_axes(): return functools.reduce(lax.psum, axes, x)  38.7 us
    unnamed x9, local copies, waits for them, and re-layouts  20 us
    all_gather x2, blocking collectives, sent_together(): result = lax.all_gather(both, axis, axis=dim, tiled=True)  17.1 us
    all_to_all x1, starting transfers between devices, sum_at_owner(): lax.all_to_all(pieces, axis, split_axis=0, concat_axis=0, tiled=True)  14.3 us
    all_gather x1, blocking collectives, gather_in_order(): pieces = lax.all_gather(pieces, axes[k], axis=0, tiled=True)  10.6 us
  transfers between devices with their start and end apart: 3, of which 3 were waited for; matrix products, arithmetic and copies ran while one was open for 1% of the time, Pallas kernels for 0%

commit v1 on v0

v1 whole, which is shorter than its diff:
```python
import functools

import jax
import jax.numpy as jnp
from jax import lax
from jax.experimental import pallas as pl
from jax.experimental.pallas import tpu as pltpu
from jax.sharding import Mesh
from jax.sharding import PartitionSpec as P

BLOCK = 2048
STEP = 10
MESH = pl.DeviceIdType.MESH
F32 = jnp.float32
BF16 = jnp.bfloat16

V = 128
D = 8192
HALF = 4096
WIDE = 1024
SUB = 256
NX, NY, NZ, NC = 4, 4, 8, 2
TILE = 16
SEMS = 256


def mod(a, n):
    return lax.rem(a + n, n)


def col(value, step):
    return pl.multiple_of(value, step)


def adam(moment, second, scaled, master):
    m2 = 0.9 * moment + 0.1 * scaled
    v2 = 0.95 * second + 0.05 * scaled * scaled
    update = m2 / (1.0 - 0.9**STEP) / (jnp.sqrt(v2 / (1.0 - 0.95**STEP)) + 1e-08)
    return m2, v2, master - 0.01 * update


def kernel(
    part_in, master_in, mc_in, vc_in, ms_in, vs_in,
    o_master, o_mc, o_vc, o_ms, o_vs, o_w,
    own, par, rcv1, snd, rcv2, s_buf, p2a, p2s, p2f, t_buf, z_buf, g_buf,
    nz, nxc, ny,
    e_master, e_mc, e_vc, e_s, sc_stage, mt, vt, wt,
    q_s, q_r, g_full,
    wbuf, l_master, l_mc, l_vc, l_ms, l_vs, r_master, r_mc, r_vc, r_ms, r_vs,
    ssem, rsem, lsem,
):
    x, y, z, c = (lax.axis_index(a) for a in ("x", "y", "z", "c"))
    other = 1 - c
    started, counts = [], [0, 0]

    def send(src, dst, **dev):
        k = counts[0]
        counts[0] += 1
        copy = pltpu.make_async_remote_copy(
            src_ref=src, dst_ref=dst, send_sem=ssem.at[k], recv_sem=rsem.at[k],
            device_id=dev, device_id_type=MESH,
        )
        copy.start()
        started.append(copy)
        return copy

    def local(src, dst):
        k = counts[1]
        counts[1] += 1
        copy = pltpu.make_async_copy(src, dst, lsem.at[k])
        copy.start()
        return copy

    axes = (("x", x, "y", y), ("y", y, "x", x))
    roles = [tuple(mod(i + d, 4) for d in (1, -1, 0, 2)) for _, i, _, _ in axes]
    roles2 = [tuple(mod(j + d, 4) for d in (1, -1, 0, 2)) for _, _, _, j in axes]
    own_k = 2 * x + c

    own_loads = [[None] * 3 for _ in range(2)]
    for role in range(3):
        for p in range(2):
            cols = pl.ds(col(p * HALF + roles[p][role] * WIDE, WIDE), WIDE)
            own_loads[p][role] = local(part_in.at[0, 0, c, :, cols], own.at[p, role])
    state_loads = [
        local(a, b)
        for a, b in (
            (ms_in, l_ms), (vs_in, l_vs), (master_in, l_master), (mc_in, l_mc), (vc_in, l_vc),
        )
    ]

    barrier = pltpu.get_barrier_semaphore()
    peers = []
    for d in range(1, 8):
        k = mod(own_k + d, 8)
        peers.append({"x": k // 2, "c": lax.rem(k, 2)})
    for d in range(1, 4):
        peers.append({"y": mod(y + d, 4)})
    for d in (1, -1):
        peers.append({"y": mod(y + d, 4), "c": other})
    for d in range(1, 8):
        peers.append({"z": mod(z + d, 8)})
    for dev in peers:
        pl.semaphore_signal(barrier, inc=1, device_id=dev, device_id_type=MESH)
    pl.semaphore_wait(barrier, len(peers))

    raw = [[[None] * 2 for _ in range(2)] for _ in range(2)]
    for q in range(2):
        m = lax.rem(c + q, 2)
        for p in range(2):
            axis = axes[p][0]
            for h in range(2):
                cols = pl.ds(col(p * HALF + roles[p][3] * WIDE + h * (WIDE // 2), WIDE // 2), WIDE // 2)
                raw[p][h][q] = send(
                    part_in.at[0, 0, m, :, cols], rcv1.at[p, h, q], **{axis: roles[p][h], "c": m}
                )
    pair = [[None] * 3 for _ in range(2)]
    for role in range(3):
        for p in range(2):
            cols = pl.ds(col(p * HALF + roles[p][role] * WIDE, WIDE), WIDE)
            pair[p][role] = send(part_in.at[0, 0, other, :, cols], par.at[p, role], c=other)

    ex = []
    tile_cols = [
        lambda kx: col(kx * WIDE + y * SUB, SUB),
        lambda kx: col(HALF + y * WIDE + kx * SUB, SUB),
    ]
    for d in range(8):
        k = mod(own_k + d, 8)
        kx, kc = k // 2, lax.rem(k, 2)
        for src, dst in ((master_in, e_master), (mc_in, e_mc), (vc_in, e_vc)):
            for p in range(2):
                s = src.at[kc, :, pl.ds(tile_cols[p](kx), SUB)]
                t = dst.at[own_k, p]
                if d == 0:
                    ex.append(local(s, t))
                else:
                    ex.append(send(s, t, x=kx, c=kc))

    plain = [[None] * 2 for _ in range(2)]
    for p in range(2):
        axis = axes[p][0]
        for side in range(2):
            own_loads[p][side].wait()
            pair[p][side].wait_recv()
            h = 1 - side
            lo = h * (WIDE // 2)

            @pl.loop(0, V // TILE)
            def _(t):
                rows = pl.ds(pl.multiple_of(t * TILE, TILE), TILE)
                cc = pl.ds(lo, WIDE // 2)
                snd[p, side, rows, cc] = own[p, side, rows, cc].astype(F32) + par[p, side, rows, cc].astype(F32)

            cc = pl.ds(lo, WIDE // 2)
            plain[p][side] = send(snd.at[p, side, :, cc], rcv2.at[p, side, :, cc], **{axis: roles[p][side]})

    for load in state_loads:
        load.wait()
    sc_stage[...] = jnp.zeros_like(sc_stage)
    for m in range(2):
        sc_stage[m, 0:2, 0:4] = l_ms[m]
        sc_stage[m, 2:4, 0:4] = l_vs[m]
    e_s[own_k] = sc_stage[c]
    for d in range(1, 8):
        k = mod(own_k + d, 8)
        kx, kc = k // 2, lax.rem(k, 2)
        ex.append(send(sc_stage.at[kc], e_s.at[own_k], x=kx, c=kc))

    relay = [[None] * 2 for _ in range(2)]
    for p in range(2):
        axis = axes[p][0]
        for side in range(2):
            h = side
            lo = h * (WIDE // 2)
            for q in range(2):
                raw[p][h][q].wait_recv()

            @pl.loop(0, V // TILE)
            def _(t):
                rows = pl.ds(pl.multiple_of(t * TILE, TILE), TILE)
                cc = pl.ds(lo, WIDE // 2)
                near = own[p, side, rows, cc].astype(F32) + par[p, side, rows, cc].astype(F32)
                far = rcv1[p, h, 0, rows, :].astype(F32) + rcv1[p, h, 1, rows, :].astype(F32)
                snd[p, side, rows, cc] = near + far

            cc = pl.ds(lo, WIDE // 2)
            relay[p][side] = send(snd.at[p, side, :, cc], rcv2.at[p, side, :, cc], **{axis: roles[p][side]})

    for copy in ex:
        copy.wait_recv()
    blocks = (x // 2, 2 + y // 2)
    for k in range(8):
        e = e_s[k]
        lane = lax.broadcasted_iota(jnp.int32, e.shape, 1)
        for p in range(2):
            scale = jnp.sum(jnp.where(lane == blocks[p], e, 0.0), axis=1, keepdims=True)
            rows = pl.ds(2 * k, 2)
            mt[p, rows, :] = e_mc[k, p].astype(F32) * scale[0:2]
            vt[p, rows, :] = e_vc[k, p].astype(F32) * scale[2:4]
            wt[p, rows, :] = e_master[k, p]

    half = SUB // 2
    for p in range(2):
        axis2 = axes[p][2]
        own_loads[p][2].wait()
        pair[p][2].wait_recv()
        for side in range(2):
            plain[p][side].wait_recv()
            relay[p][side].wait_recv()

        @pl.loop(0, V // TILE)
        def _(t):
            rows = pl.ds(pl.multiple_of(t * TILE, TILE), TILE)
            near = own[p, 2, rows, :].astype(F32) + par[p, 2, rows, :].astype(F32)
            s_buf[p, rows, :] = near + rcv2[p, 0, rows, :] + rcv2[p, 1, rows, :]

    first2 = [[None] * 2 for _ in range(2)]
    plain2 = [[None] * 2 for _ in range(2)]
    relay2 = [[None] * 2 for _ in range(2)]
    for p in range(2):
        axis2 = axes[p][2]
        r2 = roles2[p]
        for h in range(2):
            cols = pl.ds(col(r2[3] * SUB + h * half, half), half)
            first2[p][h] = send(s_buf.at[p, :, cols], p2a.at[p, h], **{axis2: r2[h]})
        for side in range(2):
            h = 1 - side
            cols = pl.ds(col(r2[side] * SUB + h * half, half), half)
            plain2[p][side] = send(s_buf.at[p, :, cols], p2f.at[p, side, h], **{axis2: r2[side]})
    for p in range(2):
        axis2 = axes[p][2]
        r2 = roles2[p]
        for side in range(2):
            h = side
            cols = pl.ds(col(r2[side] * SUB + h * half, half), half)
            first2[p][h].wait_recv()
            p2s[p, side] = s_buf[p, :, cols] + p2a[p, h]
            relay2[p][side] = send(p2s.at[p, side], p2f.at[p, side, h], **{axis2: r2[side]})
    zc = [[None] * 8 for _ in range(2)]
    for p in range(2):
        r2 = roles2[p]
        for side in range(2):
            plain2[p][side].wait_recv()
            relay2[p][side].wait_recv()
        for h in range(2):
            cols = pl.ds(col(r2[2] * SUB + h * half, half), half)
            t_buf[p, :, h * half:(h + 1) * half] = s_buf[p, :, cols] + p2f[p, 0, h] + p2f[p, 1, h]
        for d in (4, 3, 5, 2, 6, 1, 7):
            zd = mod(z + d, 8)
            rows = pl.ds(pl.multiple_of(zd * TILE, TILE), TILE)
            zc[p][d] = send(t_buf.at[p, rows, :], z_buf.at[p, d], z=zd)

    my_rows = pl.ds(pl.multiple_of(z * TILE, TILE), TILE)
    square = jnp.zeros((8, 128), F32)
    for p in range(2):
        g = t_buf[p, my_rows, :]
        for d in range(1, 8):
            zc[p][d].wait_recv()
            g = g + z_buf[p, d]
        g_buf[p] = g
        sq = g * g
        for i in range(2):
            for j in range(2):
                square = square + sq[8 * i:8 * i + 8, 128 * j:128 * j + 128]
    nz[z] = square
    n1 = [send(nz.at[z], nz.at[z], z=mod(z + d, 8)) for d in (4, 3, 5, 2, 6, 1, 7)]

    for p in range(2):
        for k in range(8):
            q_s[k, p] = g_buf[p, 2 * k:2 * k + 2, :]
    q1 = []
    for d in range(1, 8):
        k = mod(own_k + d, 8)
        q1.append(send(q_s.at[k], q_r.at[own_k], x=k // 2, c=lax.rem(k, 2)))
    q_r[own_k] = q_s[own_k]

    for copy in n1:
        copy.wait_recv()
    nxc[own_k] = functools.reduce(lambda a, b: a + b, [nz[k] for k in range(8)])
    n2 = []
    for d in range(1, 8):
        k = mod(own_k + d, 8)
        n2.append(send(nxc.at[own_k], nxc.at[own_k], x=k // 2, c=lax.rem(k, 2)))

    for copy in q1:
        copy.wait_recv()
    q2 = [send(q_r, g_full.at[y], y=mod(y + d, 4)) for d in range(1, 4)]
    g_full[y] = q_r[...]

    for copy in n2:
        copy.wait_recv()
    ny[y] = functools.reduce(lambda a, b: a + b, [nxc[k] for k in range(8)])
    n3 = [send(ny.at[y], ny.at[y], y=mod(y + d, 4)) for d in (2, 1, 3)]
    for copy in n3:
        copy.wait_recv()
    total = functools.reduce(lambda a, b: a + b, [ny[k] for k in range(4)])
    total = jnp.sum(jnp.sum(total, axis=1, keepdims=True), axis=0, keepdims=True)
    clip = 1.0 / jnp.maximum(jnp.sqrt(total), 1.0)

    block_of = lambda p, i, j: pl.ds(col(p * HALF + i * WIDE + j * SUB, SUB), SUB)
    for p in range(2):
        i1, i2 = axes[p][1], axes[p][3]
        _, _, fresh = adam(mt[p], vt[p], clip * g_buf[p], wt[p])
        wbuf[c, my_rows, block_of(p, i1, i2)] = fresh.astype(BF16)
    ag1 = [[], []]
    for d in (4, 3, 5, 2, 6, 1, 7):
        for p in range(2):
            ref = wbuf.at[c, my_rows, block_of(p, axes[p][1], axes[p][3])]
            ag1[p].append(send(ref, ref, z=mod(z + d, 8)))

    for copy in q2:
        copy.wait_recv()
    lane4 = lax.broadcasted_iota(jnp.int32, (2, 4), 1)
    for m in range(2):
        tops_m = jnp.zeros((2, 4), F32)
        tops_v = jnp.zeros((2, 4), F32)
        for b in range(4):
            cs = slice(b * BLOCK, (b + 1) * BLOCK)
            pieces = []
            for s in range(8):
                if b < 2:
                    px, py, p = 2 * b + s // 4, s % 4, 0
                else:
                    py, px, p = 2 * (b - 2) + s // 4, s % 4, 1
                pieces.append(g_full[py, 2 * px + m, p])
            g = jnp.concatenate(pieces, axis=1)
            moment = l_mc[m, :, cs].astype(F32) * l_ms[m, :, b:b + 1]
            second = l_vc[m, :, cs].astype(F32) * l_vs[m, :, b:b + 1]
            m2, v2, fresh = adam(moment, second, clip * g, l_master[m, :, cs])
            m_top = jnp.max(jnp.abs(m2), axis=1, keepdims=True) + 1e-20
            v_top = jnp.max(jnp.abs(v2), axis=1, keepdims=True) + 1e-20
            r_master[m, :, cs] = fresh
            r_mc[m, :, cs] = (m2 / m_top).astype(BF16)
            r_vc[m, :, cs] = (v2 / v_top).astype(BF16)
            tops_m = jnp.where(lane4 == b, m_top, tops_m)
            tops_v = jnp.where(lane4 == b, v_top, tops_v)
        r_ms[m] = tops_m
        r_vs[m] = tops_v
    outs = [
        local(a, b)
        for a, b in (
            (r_master, o_master), (r_mc, o_mc), (r_vc, o_vc), (r_ms, o_ms), (r_vs, o_vs),
        )
    ]

    to_pair, to_out = [], []
    rows_half = (pl.ds(0, V // 2), pl.ds(V // 2, V // 2))

    def finished(p, i, j):
        ref = wbuf.at[c, :, block_of(p, i, j)]
        to_pair.append((send(ref, ref, c=other), wbuf.at[other, :, block_of(p, i, j)],
                        o_w.at[other, :, block_of(p, i, j)]))
        to_out.append(local(ref, o_w.at[c, :, block_of(p, i, j)]))

    def spread(p, i, j, axis, targets):
        ref = wbuf.at[c, :, block_of(p, i, j)]
        return [send(ref, ref, **{axis: targets[side]}) for side in range(2)]

    def forward(p, i, j, axis, target, h):
        ref = wbuf.at[c, rows_half[h], block_of(p, i, j)]
        return send(ref, ref, **{axis: target})

    second_axis, first_axis, fwd2 = [None] * 2, [[None] * 4 for _ in range(2)], [None] * 2
    for p in range(2):
        a1, i1, a2, i2 = axes[p]
        for copy in ag1[p]:
            copy.wait_recv()
        second_axis[p] = spread(p, i1, i2, a2, roles2[p])
        first_axis[p][0] = spread(p, i1, i2, a1, roles[p])
        finished(p, i1, i2)
    for p in range(2):
        a1, i1, a2, i2 = axes[p]
        right2, left2, _, opp2 = roles2[p]
        fwd2[p] = []
        for side, origin in ((0, left2), (1, right2)):
            second_axis[p][side].wait_recv()
            fwd2[p].append(forward(p, i1, origin, a2, roles2[p][side], side))
            first_axis[p][1 + side] = spread(p, i1, origin, a1, roles[p])
            finished(p, i1, origin)

    fwd1 = [[None] * 4 for _ in range(2)]

    def pass_on(p, s):
        a1, i1, a2, i2 = axes[p]
        right1, left1, _, _ = roles[p]
        right2, left2, _, opp2 = roles2[p]
        j = (i2, left2, right2, opp2)[s]
        fwd1[p][s] = []
        for side, origin in ((0, left1), (1, right1)):
            first_axis[p][s][side].wait_recv()
            fwd1[p][s].append(forward(p, origin, j, a1, roles[p][side], side))
            finished(p, origin, j)

    def complete(p, s):
        a1, i1, a2, i2 = axes[p]
        right2, left2, _, opp2 = roles2[p]
        j = (i2, left2, right2, opp2)[s]
        for copy in fwd1[p][s]:
            copy.wait_recv()
        finished(p, roles[p][3], j)

    for p in range(2):
        pass_on(p, 0)
    for p in range(2):
        a1, i1, a2, i2 = axes[p]
        for copy in fwd2[p]:
            copy.wait_recv()
        first_axis[p][3] = spread(p, i1, roles2[p][3], a1, roles[p])
        finished(p, i1, roles2[p][3])
    for s in range(1, 4):
        for p in range(2):
            pass_on(p, s)
            complete(p, s - 1)
    for p in range(2):
        complete(p, 3)

    for copy, src, dst in to_pair:
        copy.wait_recv()
        to_out.append(local(src, dst))
    for copy in to_out + outs:
        copy.wait()
    for copy in started:
        copy.wait_send()
    assert counts[0] <= SEMS and counts[1] <= 128, counts


def body(partials, master, m_codes, v_codes, m_scales, v_scales):
    any_spec = pl.BlockSpec(memory_space=pl.ANY)
    vmem = pltpu.VMEM
    return pl.pallas_call(
        kernel,
        out_shape=(
            jax.ShapeDtypeStruct(master.shape, F32),
            jax.ShapeDtypeStruct(master.shape, BF16),
            jax.ShapeDtypeStruct(master.shape, BF16),
            jax.ShapeDtypeStruct(m_scales.shape, F32),
            jax.ShapeDtypeStruct(m_scales.shape, F32),
            jax.ShapeDtypeStruct((2, V, D), BF16),
        ),
        in_specs=[any_spec] * 6,
        out_specs=(any_spec,) * 6,
        scratch_shapes=[
            vmem((2, 3, V, WIDE), BF16),
            vmem((2, 3, V, WIDE), BF16),
            vmem((2, 2, 2, V, WIDE // 2), BF16),
            vmem((2, 2, V, WIDE), F32),
            vmem((2, 2, V, WIDE), F32),
            vmem((2, V, WIDE), F32),
            vmem((2, 2, V, SUB // 2), F32),
            vmem((2, 2, V, SUB // 2), F32),
            vmem((2, 2, 2, V, SUB // 2), F32),
            vmem((2, V, SUB), F32),
            vmem((2, 8, TILE, SUB), F32),
            vmem((2, TILE, SUB), F32),
            vmem((8, 8, 128), F32),
            vmem((8, 8, 128), F32),
            vmem((4, 8, 128), F32),
            vmem((8, 2, 2, SUB), F32),
            vmem((8, 2, 2, SUB), BF16),
            vmem((8, 2, 2, SUB), BF16),
            vmem((8, 4, 128), F32),
            vmem((2, 4, 128), F32),
            vmem((2, TILE, SUB), F32),
            vmem((2, TILE, SUB), F32),
            vmem((2, TILE, SUB), F32),
            vmem((8, 2, 2, SUB), F32),
            vmem((8, 2, 2, SUB), F32),
            vmem((4, 8, 2, 2, SUB), F32),
            vmem((2, V, D), BF16),
            vmem((2, 2, D), F32),
            vmem((2, 2, D), BF16),
            vmem((2, 2, D), BF16),
            vmem((2, 2, 4), F32),
            vmem((2, 2, 4), F32),
            vmem((2, 2, D), F32),
            vmem((2, 2, D), BF16),
            vmem((2, 2, D), BF16),
            vmem((2, 2, 4), F32),
            vmem((2, 2, 4), F32),
            pltpu.SemaphoreType.DMA((SEMS,)),
            pltpu.SemaphoreType.DMA((SEMS,)),
            pltpu.SemaphoreType.DMA((128,)),
        ],
        compiler_params=pltpu.CompilerParams(
            collective_id=0, has_side_effects=True, vmem_limit_bytes=48 * 1024 * 1024
        ),
        name="step",
    )(partials, master, m_codes, v_codes, m_scales, v_scales)


def solution(mesh):
    finer = Mesh(mesh.devices.reshape(NZ, NX, NC, NY), ("z", "x", "c", "y"))
    rows = P(None, ("z", "x", "c"), None)
    return jax.shard_map(
        body,
        mesh=finer,
        in_specs=(P("y", ("z", "x", "c"), None, None, None),) + (rows,) * 5,
        out_specs=(rows,) * 5 + (P(),),
        check_vma=False,
    )
```

time: 305 us -> 96.6 us (0.32); the launches traced: 301 us -> 96.4 us
  blocking collectives: 128 us -> 0 us
  waiting for transfers between devices: 94 us -> 0 us
  Pallas kernels: 0 us -> 86.7 us
  local copies, waits for them, and re-layouts: 42 us -> 9.02 us
  starting transfers between devices: 14.4 us -> 0 us
  between operations: 14.8 us -> 0.66 us
  other arithmetic: 8.43 us -> 0 us
    pallas_call x0 -> x1, Pallas kernels: none -> 86.7 us  [body(): pl.pallas_call(kernel, out_shape=(jax.ShapeDtypeStruct(master.shape, F32)...]
    all_to_all x1 -> x0, blocking collectives: 51.9 us -> none  [body(): lax.all_to_all(own_terms[None], 'outer', split_axis=3, concat_axis=0, til...]
    all_to_all x1 -> x0, waiting for transfers between devices: 49.5 us -> none  [sum_at_owner(): lax.all_to_all(pieces, axis, split_axis=0, concat_axis=0, tiled=True)]
    all_gather x2 -> x0, waiting for transfers between devices: 44.5 us -> none  [gather_in_order(): pieces = lax.all_gather(pieces, axes[k], axis=0, tiled=True)]
    psum x4 -> x0, blocking collectives: 38.7 us -> none  [over_axes(): return functools.reduce(lax.psum, axes, x)]
    all_gather x4 -> x0, blocking collectives: 37 us -> none  [the longest x2 17.1 us: sent_together(): result = lax.all_gather(both, axis, axis=dim, tiled=True)]
    all_to_all x1 -> x0, starting transfers between devices: 14.3 us -> none  [sum_at_owner(): lax.all_to_all(pieces, axis, split_axis=0, concat_axis=0, tiled=True)]
    transpose x2 -> x0, local copies, waits for them, and re-layouts: 11.2 us -> none  [the longest x1 6.28 us: in_order(): return jnp.moveaxis(pieces, 0, dim).reshape(lengths)]
  transfers between devices with their start and end apart: 3 -> 0, of which waited for: 3 -> 0; matrix products, arithmetic and copies ran while one was open for 1% -> 0% of each run, Pallas kernels for 0% -> 0%
where the time goes in v1:
time: 96.6 us; the launch traced here: 96.4 us
  Pallas kernels  86.7 us (90%)
  local copies, waits for them, and re-layouts  9.02 us (9%)
    pallas_call x1, Pallas kernels, body(): pl.pallas_call(kernel, out_shape=(jax.ShapeDtypeStruct(master.shape, F32)...  86.7 us
    unnamed x16, local copies, waits for them, and re-layouts  9.02 us

profile of v1, /device:TPU:1, one launch (start us, length us, event | category | flops | bytes accessed | tf_op | source)
XLA Modules:
  0.0 96.4 jit_solution(15900171589283636854)
XLA Ops:
  0.6 0.0 copy-start
  0.6 0.9 copy-done
  1.5 0.0 copy-start.1
  1.5 0.8 copy-done.1
  2.4 0.0 copy-start.2
  2.4 0.8 copy-done.2
  3.2 0.0 copy-start.3
  3.2 0.7 copy-done.3
  3.9 0.0 copy-start.4
  3.9 0.7 copy-done.4
  4.6 86.7 %step.1 = (f32[2,2,8192]{2,1,0:T(2,128)S(1)}, bf16[2,2,8192]{2,1,0:T(2,128)(2,1)S(1)}, bf16[2,2,8192]{2,1,0:T(2,128)(2,1)S(1)}, f32[2,2,4]{2,1,0:T(2,128)S(1)}, ...) custom-call(bf16[1,1,2,128,8192]{4,3,2,1,0:T(8,128)(2,1)} %part_in.1, f32[2,2,8192]{2,1,0:T(2,128)S(1)} %copy-done, ...), custom_call_target="tpu_custom_call" | custom-call | tf_op jit(solution)/shard_map/step/pallas_call | solution.py:430
  91.3 0.7 copy.18
  92.0 0.6 copy.19
  92.6 0.6 copy.20
  93.2 0.6 copy.21
  93.8 0.6 copy.22
  94.4 2.0 %copy.23 = bf16[2,128,8192]{2,1,0:T(8,128)(2,1)} copy(bf16[2,128,8192]{2,1,0:T(8,128)(2,1)S(1)} %get-tuple-element.17) | data formatting | bytes 8388608
Async XLA Ops:
  0.6 0.9 copy-start
  1.5 0.8 copy-start.1
  2.4 0.8 copy-start.2
  3.2 0.7 copy-start.3
  3.9 0.7 copy-start.4

commit v2 on v1

--- a/solution.py
+++ b/solution.py
@@ -46,12 +46,13 @@
     nz, nxc, ny,
     e_master, e_mc, e_vc, e_s, sc_stage, mt, vt, wt,
     q_s, q_r, g_full,
-    wbuf, l_master, l_mc, l_vc, l_ms, l_vs, r_master, r_mc, r_vc, r_ms, r_vs,
+    l_master, l_mc, l_vc, l_ms, l_vs,
     ssem, rsem, lsem,
 ):
     x, y, z, c = (lax.axis_index(a) for a in ("x", "y", "z", "c"))
     other = 1 - c
     started, counts = [], [0, 0]
+
 
     def send(src, dst, **dev):
         k = counts[0]
@@ -301,11 +302,11 @@
     for p in range(2):
         i1, i2 = axes[p][1], axes[p][3]
         _, _, fresh = adam(mt[p], vt[p], clip * g_buf[p], wt[p])
-        wbuf[c, my_rows, block_of(p, i1, i2)] = fresh.astype(BF16)
+        o_w[c, my_rows, block_of(p, i1, i2)] = fresh.astype(BF16)
     ag1 = [[], []]
     for d in (4, 3, 5, 2, 6, 1, 7):
         for p in range(2):
-            ref = wbuf.at[c, my_rows, block_of(p, axes[p][1], axes[p][3])]
+            ref = o_w.at[c, my_rows, block_of(p, axes[p][1], axes[p][3])]
             ag1[p].append(send(ref, ref, z=mod(z + d, 8)))
 
     for copy in q2:
@@ -329,35 +330,27 @@
             m2, v2, fresh = adam(moment, second, clip * g, l_master[m, :, cs])
             m_top = jnp.max(jnp.abs(m2), axis=1, keepdims=True) + 1e-20
             v_top = jnp.max(jnp.abs(v2), axis=1, keepdims=True) + 1e-20
-            r_master[m, :, cs] = fresh
-            r_mc[m, :, cs] = (m2 / m_top).astype(BF16)
-            r_vc[m, :, cs] = (v2 / v_top).astype(BF16)
+            o_master[m, :, cs] = fresh
+            o_mc[m, :, cs] = (m2 / m_top).astype(BF16)
+            o_vc[m, :, cs] = (v2 / v_top).astype(BF16)
             tops_m = jnp.where(lane4 == b, m_top, tops_m)
             tops_v = jnp.where(lane4 == b, v_top, tops_v)
-        r_ms[m] = tops_m
-        r_vs[m] = tops_v
-    outs = [
-        local(a, b)
-        for a, b in (
-            (r_master, o_master), (r_mc, o_mc), (r_vc, o_vc), (r_ms, o_ms), (r_vs, o_vs),
-        )
-    ]
-
-    to_pair, to_out = [], []
+        o_ms[m] = tops_m
+        o_vs[m] = tops_v
+
+    to_pair = []
     rows_half = (pl.ds(0, V // 2), pl.ds(V // 2, V // 2))
 
     def finished(p, i, j):
-        ref = wbuf.at[c, :, block_of(p, i, j)]
-        to_pair.append((send(ref, ref, c=other), wbuf.at[other, :, block_of(p, i, j)],
-                        o_w.at[other, :, block_of(p, i, j)]))
-        to_out.append(local(ref, o_w.at[c, :, block_of(p, i, j)]))
+        ref = o_w.at[c, :, block_of(p, i, j)]
+        to_pair.append(send(ref, ref, c=other))
 
     def spread(p, i, j, axis, targets):
-        ref = wbuf.at[c, :, block_of(p, i, j)]
+        ref = o_w.at[c, :, block_of(p, i, j)]
         return [send(ref, ref, **{axis: targets[side]}) for side in range(2)]
 
     def forward(p, i, j, axis, target, h):
-        ref = wbuf.at[c, rows_half[h], block_of(p, i, j)]
+        ref = o_w.at[c, rows_half[h], block_of(p, i, j)]
         return send(ref, ref, **{axis: target})
 
     second_axis, first_axis, fwd2 = [None] * 2, [[None] * 4 for _ in range(2)], [None] * 2
@@ -414,20 +407,27 @@
     for p in range(2):
         complete(p, 3)
 
-    for copy, src, dst in to_pair:
-        copy.wait_recv()
-        to_out.append(local(src, dst))
-    for copy in to_out + outs:
-        copy.wait()
+    for copy in to_pair:
+        copy.wait_recv()
     for copy in started:
         copy.wait_send()
     assert counts[0] <= SEMS and counts[1] <= 128, counts
 
 
+def write_out(*refs):
+    sems = refs[12]
+    copies = [pltpu.make_async_copy(refs[k], refs[k + 6], sems.at[k]) for k in (5, 0, 1, 2, 3, 4)]
+    for copy in copies:
+        copy.start()
+    for copy in copies:
+        copy.wait()
+
+
 def body(partials, master, m_codes, v_codes, m_scales, v_scales):
     any_spec = pl.BlockSpec(memory_space=pl.ANY)
     vmem = pltpu.VMEM
-    return pl.pallas_call(
+    small = [pltpu.with_memory_space_constraint(a, pltpu.HBM) for a in (master, m_codes, v_codes, m_scales, v_scales)]
+    results = pl.pallas_call(
         kernel,
         out_shape=(
             jax.ShapeDtypeStruct(master.shape, F32),
@@ -437,8 +437,8 @@
             jax.ShapeDtypeStruct(m_scales.shape, F32),
             jax.ShapeDtypeStruct((2, V, D), BF16),
         ),
-        in_specs=[any_spec] * 6,
-        out_specs=(any_spec,) * 6,
+        in_specs=[pl.BlockSpec(memory_space=pltpu.HBM)] * 6,
+        out_specs=(pl.BlockSpec(memory_space=pltpu.VMEM),) * 6,
         scratch_shapes=[
             vmem((2, 3, V, WIDE), BF16),
             vmem((2, 3, V, WIDE), BF16),
@@ -466,12 +466,6 @@
             vmem((8, 2, 2, SUB), F32),
             vmem((8, 2, 2, SUB), F32),
             vmem((4, 8, 2, 2, SUB), F32),
-            vmem((2, V, D), BF16),
-            vmem((2, 2, D), F32),
-            vmem((2, 2, D), BF16),
-            vmem((2, 2, D), BF16),
-            vmem((2, 2, 4), F32),
-            vmem((2, 2, 4), F32),
             vmem((2, 2, D), F32),
             vmem((2, 2, D), BF16),
             vmem((2, 2, D), BF16),
@@ -485,7 +479,16 @@
             collective_id=0, has_side_effects=True, vmem_limit_bytes=48 * 1024 * 1024
         ),
         name="step",
-    )(partials, master, m_codes, v_codes, m_scales, v_scales)
+    )(partials, *small)
+    return pl.pallas_call(
+        write_out,
+        out_shape=tuple(jax.ShapeDtypeStruct(a.shape, a.dtype) for a in results),
+        in_specs=[any_spec] * 6,
+        out_specs=(any_spec,) * 6,
+        scratch_shapes=[pltpu.SemaphoreType.DMA((6,))],
+        compiler_params=pltpu.CompilerParams(vmem_limit_bytes=1024 * 1024),
+        name="write_out",
+    )(*results)
 
 
 def solution(mesh):

time: 96.6 us -> 89.3 us (0.924)
  local copies, waits for them, and re-layouts: 9.02 us -> 0 us
  Pallas kernels: 86.7 us -> 88.6 us
    unnamed x16 -> x0, local copies, waits for them, and re-layouts: 9.02 us -> none
    pallas_call x0 -> x1, Pallas kernels: none -> 2.13 us  [body(): pl.pallas_call(write_out, out_shape=tuple((jax.ShapeDtypeStruct(a.shape,...]
where the time goes in v2:
time: 89.3 us; the launch traced here: 89.2 us
  Pallas kernels  88.6 us (99%)
    pallas_call x1, Pallas kernels, body(): pl.pallas_call(kernel, out_shape=(jax.ShapeDtypeStruct(master.shape, F32)...  86.4 us
    pallas_call x1, Pallas kernels, body(): pl.pallas_call(write_out, out_shape=tuple((jax.ShapeDtypeStruct(a.shape,...  2.13 us

profile of v2, /device:TPU:1, one launch (start us, length us, event | category | flops | bytes accessed | tf_op | source)
XLA Modules:
  0.0 89.2 jit_solution(7122078942139953161)
XLA Ops:
  0.6 86.4 %step.1 = (f32[2,2,8192]{2,1,0:T(2,128)S(1)}, bf16[2,2,8192]{2,1,0:T(2,128)(2,1)S(1)}, bf16[2,2,8192]{2,1,0:T(2,128)(2,1)S(1)}, f32[2,2,4]{2,1,0:T(2,128)S(1)}, ...) custom-call(bf16[1,1,2,128,8192]{4,3,2,1,0:T(8,128)(2,1)} %part_in.1, f32[2,2,8192]{2,1,0:T(2,128)} %master_in.1, ...), custom_call_target="tpu_custom_call" | custom-call | tf_op jit(solution)/shard_map/step/pallas_call | solution.py:430
  87.1 2.1 %write_out.1 = (f32[2,2,8192]{2,1,0:T(2,128)}, bf16[2,2,8192]{2,1,0:T(2,128)(2,1)}, bf16[2,2,8192]{2,1,0:T(2,128)(2,1)}, f32[2,2,4]{2,1,0:T(2,128)}, f32[2,2,4]{2,1,0:T(2,128)}, /*index=5*/bf16[2,128,8192]{2,1,0:T(8,128)(2,1)}) custom-call(f32[2,2,8192]{2,1,0:T(2,128)S(1)} %get-tuple-element.12.refs_0_, bf16[2,2,8192]{2,1,0:T(2,128)(2,1)S(1)} %get-tuple-element.13.refs_1_, ...), custom_call_target="tpu_custom_call" | custom-call | tf_op jit(solution)/shard_map/write_out/pallas_call | solution.py:483

commit v3 on v2

v3 whole, which is shorter than its diff:
```python
import functools
import math

import jax
import jax.numpy as jnp
from jax import lax
from jax.experimental import pallas as pl
from jax.experimental.pallas import tpu as pltpu
from jax.sharding import Mesh
from jax.sharding import PartitionSpec as P

BLOCK = 2048
STEP = 10
MESH = pl.DeviceIdType.MESH
F32 = jnp.float32
BF16 = jnp.bfloat16

V = 128
D = 8192
HALF = 4096
WIDE = 1024
SUB = 256
NX, NY, NZ, NC = 4, 4, 8, 2
TILE = 16
SEMS = 80
LOCAL_SEMS = 18
LIMIT_KIB = 12 * 1024


def mod(a, n):
    return lax.rem(a + n, n)


def col(value, step):
    return pl.multiple_of(value, step)


def adam(moment, second, scaled, master):
    m2 = 0.9 * moment + 0.1 * scaled
    v2 = 0.95 * second + 0.05 * scaled * scaled
    update = m2 / (1.0 - 0.9**STEP) / (jnp.sqrt(v2 / (1.0 - 0.95**STEP)) + 1e-08)
    return m2, v2, master - 0.01 * update


def kernel(
    part_in, master_in, mc_in, vc_in, ms_in, vs_in,
    o_master, o_mc, o_vc, o_ms, o_vs, o_w,
    own, par, rcv1, snd, rcv2, s_buf, p2f, t_buf, z_buf, g_buf,
    nzc, nxy,
    e_master, e_mc, e_vc, e_s, sc_stage, mt, vt, wt,
    q_s, q_r, g_full,
    l_master, l_mc, l_vc, l_ms, l_vs, bytes_ref,
    ssem, rsem, lsem,
):
    x, y, z, c = (lax.axis_index(a) for a in ("x", "y", "z", "c"))
    other = 1 - c
    groups, sent = [0, 0], [0]

    def size(ref):
        return math.prod(ref.shape) * ref.dtype.itemsize // 1024

    def group():
        groups[0] += 1
        return groups[0] - 1

    def send(src, dst, k, **dev):
        sent[0] += size(src)
        pltpu.make_async_remote_copy(
            src_ref=src, dst_ref=dst, send_sem=ssem.at[0], recv_sem=rsem.at[k],
            device_id=dev, device_id_type=MESH,
        ).start()

    def arrived(k, kib):
        ref = bytes_ref.at[pl.ds(0, kib)]
        pltpu.make_async_copy(ref, ref, rsem.at[k]).wait()

    def all_sent():
        assert sent[0] <= LIMIT_KIB
        ref = bytes_ref.at[pl.ds(0, sent[0])]
        pltpu.make_async_copy(ref, ref, ssem.at[0]).wait()


    def local(src, dst):
        groups[1] += 1
        copy = pltpu.make_async_copy(src, dst, lsem.at[groups[1] - 1])
        copy.start()
        return copy


    axes = (("x", x, "y", y), ("y", y, "x", x))
    roles = [tuple(mod(i + d, 4) for d in (1, -1, 0, 2)) for _, i, _, _ in axes]
    roles2 = [tuple(mod(j + d, 4) for d in (1, -1, 0, 2)) for _, _, _, j in axes]
    own_k = 2 * x + c

    own_loads = [[None] * 3 for _ in range(2)]
    for role in range(3):
        for p in range(2):
            cols = pl.ds(col(p * HALF + roles[p][role] * WIDE, WIDE), WIDE)
            own_loads[p][role] = local(part_in.at[0, 0, c, :, cols], own.at[p, role])
    state_loads = [
        local(a, b)
        for a, b in (
            (ms_in, l_ms), (vs_in, l_vs), (master_in, l_master), (mc_in, l_mc), (vc_in, l_vc),
        )
    ]

    barrier = pltpu.get_barrier_semaphore()
    xc_peers, xy_peers, zc_peers = [], [], []
    for d in range(1, 8):
        k = mod(own_k + d, 8)
        xc_peers.append((k, {"x": k // 2, "c": lax.rem(k, 2)}))
    for d in (10, 9, 11, 6, 14, 2, 8, 5, 7, 13, 15, 1, 3, 4, 12):
        xy_peers.append({"x": mod(x + d // 4, 4), "y": mod(y + d % 4, 4)})
    for d in (8, 9, 6, 7, 10, 11, 4, 5, 12, 13, 2, 3, 14, 15, 1):
        zc_peers.append({"z": mod(z + d // 2, 8), "c": lax.rem(c + d % 2, 2)})
    greeted = list(xy_peers) + list(zc_peers)
    greeted += [{"x": mod(x + d, 4), "c": other} for d in (1, 2, 3)]
    greeted += [{"y": mod(y + d, 4), "c": other} for d in (1, 3)]
    for dev in greeted:
        pl.semaphore_signal(barrier, inc=1, device_id=dev, device_id_type=MESH)
    pl.semaphore_wait(barrier, len(greeted))

    raw = [[group() for _ in range(2)] for _ in range(2)]
    for q in range(2):
        m = lax.rem(c + q, 2)
        for p in range(2):
            axis = axes[p][0]
            for h in range(2):
                cols = pl.ds(col(p * HALF + roles[p][3] * WIDE + h * (WIDE // 2), WIDE // 2), WIDE // 2)
                send(part_in.at[0, 0, m, :, cols], rcv1.at[p, h, q], raw[p][h], **{axis: roles[p][h], "c": m})
    pair = [[group() for _ in range(3)] for _ in range(2)]
    for role in range(3):
        for p in range(2):
            cols = pl.ds(col(p * HALF + roles[p][role] * WIDE, WIDE), WIDE)
            send(part_in.at[0, 0, other, :, cols], par.at[p, role], pair[p][role], c=other)

    from_side = [[group() for _ in range(2)] for _ in range(2)]
    for p in range(2):
        axis = axes[p][0]
        for side in range(2):
            own_loads[p][side].wait()
            arrived(pair[p][side], size(par.at[p, side]))
            lo = (1 - side) * (WIDE // 2)

            @pl.loop(0, V // TILE)
            def _(t):
                rows = pl.ds(pl.multiple_of(t * TILE, TILE), TILE)
                cc = pl.ds(lo, WIDE // 2)
                snd[p, side, rows, cc] = own[p, side, rows, cc].astype(F32) + par[p, side, rows, cc].astype(F32)

            cc = pl.ds(lo, WIDE // 2)
            send(snd.at[p, side, :, cc], rcv2.at[p, side, :, cc], from_side[p][side], **{axis: roles[p][side]})

    state = group()
    tile_cols = [
        lambda kx: col(kx * WIDE + y * SUB, SUB),
        lambda kx: col(HALF + y * WIDE + kx * SUB, SUB),
    ]
    own_state = []
    for src, dst in ((master_in, e_master), (mc_in, e_mc), (vc_in, e_vc)):
        for p in range(2):
            own_state.append(local(src.at[c, :, pl.ds(tile_cols[p](x), SUB)], dst.at[own_k, p]))
            for k, dev in xc_peers:
                send(src.at[dev["c"], :, pl.ds(tile_cols[p](dev["x"]), SUB)], dst.at[own_k, p], state, **dev)
    for load in state_loads:
        load.wait()
    sc_stage[...] = jnp.zeros_like(sc_stage)
    for m in range(2):
        sc_stage[m, 0:2, 0:4] = l_ms[m]
        sc_stage[m, 2:4, 0:4] = l_vs[m]
    e_s[own_k] = sc_stage[c]
    for k, dev in xc_peers:
        send(sc_stage.at[dev["c"]], e_s.at[own_k], state, **dev)

    for p in range(2):
        axis = axes[p][0]
        for side in range(2):
            h = side
            lo = h * (WIDE // 2)
            arrived(raw[p][h], size(rcv1.at[p, h]))

            @pl.loop(0, V // TILE)
            def _(t):
                rows = pl.ds(pl.multiple_of(t * TILE, TILE), TILE)
                cc = pl.ds(lo, WIDE // 2)
                near = own[p, side, rows, cc].astype(F32) + par[p, side, rows, cc].astype(F32)
                far = rcv1[p, h, 0, rows, :].astype(F32) + rcv1[p, h, 1, rows, :].astype(F32)
                snd[p, side, rows, cc] = near + far

            cc = pl.ds(lo, WIDE // 2)
            send(snd.at[p, side, :, cc], rcv2.at[p, side, :, cc], from_side[p][side], **{axis: roles[p][side]})

    for copy in own_state:
        copy.wait()
    arrived(state, 7 * 10)
    blocks = (x // 2, 2 + y // 2)
    for k in range(8):
        e = e_s[k]
        lane = lax.broadcasted_iota(jnp.int32, e.shape, 1)
        for p in range(2):
            scale = jnp.sum(jnp.where(lane == blocks[p], e, 0.0), axis=1, keepdims=True)
            rows = pl.ds(2 * k, 2)
            mt[p, rows, :] = e_mc[k, p].astype(F32) * scale[0:2]
            vt[p, rows, :] = e_vc[k, p].astype(F32) * scale[2:4]
            wt[p, rows, :] = e_master[k, p]

    second = [group() for _ in range(2)]
    for p in range(2):
        axis2, r2 = axes[p][2], roles2[p]
        own_loads[p][2].wait()
        arrived(pair[p][2], size(par.at[p, 2]))
        for side in range(2):
            arrived(from_side[p][side], size(rcv2.at[p, side]))
        for n in (3, 0, 1, 2):
            cols = pl.ds(col(r2[n] * SUB, SUB), SUB)

            @pl.loop(0, V // TILE)
            def _(t):
                rows = pl.ds(pl.multiple_of(t * TILE, TILE), TILE)
                near = own[p, 2, rows, cols].astype(F32) + par[p, 2, rows, cols].astype(F32)
                s_buf[p, rows, cols] = near + rcv2[p, 0, rows, cols] + rcv2[p, 1, rows, cols]

            if n != 2:
                send(s_buf.at[p, :, cols], p2f.at[p, n if n < 2 else 2], second[p], **{axis2: r2[n]})

    third = [group() for _ in range(2)]
    for p in range(2):
        r2 = roles2[p]
        arrived(second[p], size(p2f.at[p]))
        cols = pl.ds(col(r2[2] * SUB, SUB), SUB)

        @pl.loop(0, V // TILE)
        def _(t):
            rows = pl.ds(pl.multiple_of(t * TILE, TILE), TILE)
            t_buf[p, rows, :] = s_buf[p, rows, cols] + p2f[p, 0, rows] + (p2f[p, 1, rows] + p2f[p, 2, rows])

        for d in (4, 3, 5, 2, 6, 1, 7):
            zd = mod(z + d, 8)
            rows = pl.ds(pl.multiple_of(zd * TILE, TILE), TILE)
            send(t_buf.at[p, rows, :], z_buf.at[p, d - 1], third[p], z=zd)

    my_rows = pl.ds(pl.multiple_of(z * TILE, TILE), TILE)
    square = jnp.zeros((8, 128), F32)
    for p in range(2):
        arrived(third[p], size(z_buf.at[p]))
        g = t_buf[p, my_rows, :]
        for d in range(7):
            g = g + z_buf[p, d]
        g_buf[p] = g
        sq = g * g
        for i in range(2):
            for j in range(2):
                square = square + sq[8 * i:8 * i + 8, 128 * j:128 * j + 128]
    norm_zc, norm_xy, q1, q2 = (group() for _ in range(4))
    slot = 2 * z + c
    nzc[slot] = square
    for dev in zc_peers:
        send(nzc.at[slot], nzc.at[slot], norm_zc, **dev)

    for p in range(2):
        for k in range(8):
            q_s[k, p] = g_buf[p, 2 * k:2 * k + 2, :]
    for k, dev in xc_peers:
        send(q_s.at[k], q_r.at[own_k], q1, **dev)
    q_r[own_k] = q_s[own_k]

    arrived(norm_zc, 15 * 4)
    slot = 4 * x + y
    nxy[slot] = functools.reduce(lambda a, b: a + b, [nzc[k] for k in range(16)])
    for dev in xy_peers:
        send(nxy.at[slot], nxy.at[slot], norm_xy, **dev)

    arrived(q1, 7 * 4)
    for d in (2, 1, 3):
        send(q_r, g_full.at[y], q2, y=mod(y + d, 4))
    g_full[y] = q_r[...]

    arrived(norm_xy, 15 * 4)
    total = functools.reduce(lambda a, b: a + b, [nxy[k] for k in range(16)])
    total = jnp.sum(jnp.sum(total, axis=1, keepdims=True), axis=0, keepdims=True)
    clip = 1.0 / jnp.maximum(jnp.sqrt(total), 1.0)

    block_of = lambda p, i, j: pl.ds(col(p * HALF + i * WIDE + j * SUB, SUB), SUB)
    for p in range(2):
        i1, i2 = axes[p][1], axes[p][3]
        _, _, fresh = adam(mt[p], vt[p], clip * g_buf[p], wt[p])
        o_w[c, my_rows, block_of(p, i1, i2)] = fresh.astype(BF16)
    ag1 = [group() for _ in range(2)]
    for d in (4, 3, 5, 2, 6, 1, 7):
        for p in range(2):
            ref = o_w.at[c, my_rows, block_of(p, axes[p][1], axes[p][3])]
            send(ref, ref, ag1[p], z=mod(z + d, 8))

    arrived(q2, 3 * 32)
    lane4 = lax.broadcasted_iota(jnp.int32, (2, 4), 1)
    for m in range(2):
        tops_m = jnp.zeros((2, 4), F32)
        tops_v = jnp.zeros((2, 4), F32)
        for b in range(4):
            cs = slice(b * BLOCK, (b + 1) * BLOCK)
            pieces = []
            for s in range(8):
                if b < 2:
                    px, py, p = 2 * b + s // 4, s % 4, 0
                else:
                    py, px, p = 2 * (b - 2) + s // 4, s % 4, 1
                pieces.append(g_full[py, 2 * px + m, p])
            g = jnp.concatenate(pieces, axis=1)
            moment = l_mc[m, :, cs].astype(F32) * l_ms[m, :, b:b + 1]
            second_ = l_vc[m, :, cs].astype(F32) * l_vs[m, :, b:b + 1]
            m2, v2, fresh = adam(moment, second_, clip * g, l_master[m, :, cs])
            m_top = jnp.max(jnp.abs(m2), axis=1, keepdims=True) + 1e-20
            v_top = jnp.max(jnp.abs(v2), axis=1, keepdims=True) + 1e-20
            o_master[m, :, cs] = fresh
            o_mc[m, :, cs] = (m2 / m_top).astype(BF16)
            o_vc[m, :, cs] = (v2 / v_top).astype(BF16)
            tops_m = jnp.where(lane4 == b, m_top, tops_m)
            tops_v = jnp.where(lane4 == b, v_top, tops_v)
        o_ms[m] = tops_m
        o_vs[m] = tops_v

    to_pair = group()
    rows_half = (pl.ds(0, V // 2), pl.ds(V // 2, V // 2))
    block_kib = V * SUB * 2 // 1024

    def finished(p, i, j):
        ref = o_w.at[c, :, block_of(p, i, j)]
        send(ref, ref, to_pair, c=other)

    def spread(p, i, j, axis, targets):
        ref = o_w.at[c, :, block_of(p, i, j)]
        ks = [group() for _ in targets]
        for k, target in zip(ks, targets):
            send(ref, ref, k, **{axis: target})
        return ks

    def forward(p, i, j, axis, target, h, k):
        ref = o_w.at[c, rows_half[h], block_of(p, i, j)]
        send(ref, ref, k, **{axis: target})

    along2, along1 = [None] * 2, [[None] * 4 for _ in range(2)]
    for p in range(2):
        a1, i1, a2, i2 = axes[p]
        arrived(ag1[p], 7 * TILE * SUB * 2 // 1024)
        right2, left2, _, opp2 = roles2[p]
        along2[p] = spread(p, i1, i2, a2, (opp2, right2, left2))
        along1[p][0] = spread(p, i1, i2, a1, roles[p][:2])
        finished(p, i1, i2)
    for n, s in ((1, 1), (2, 2), (0, 3)):
        for p in range(2):
            a1, i1, a2, i2 = axes[p]
            right2, left2, _, opp2 = roles2[p]
            origin = (opp2, left2, right2)[n]
            arrived(along2[p][n], block_kib)
            targets = roles[p][:2] if s < 3 else (roles[p][3],) + roles[p][:2]
            along1[p][s] = spread(p, i1, origin, a1, targets)
            finished(p, i1, origin)

    fwd1 = [[group() for _ in range(3)] for _ in range(2)]

    def column(p, s):
        right2, left2, _, opp2 = roles2[p]
        return (axes[p][3], left2, right2, opp2)[s]

    def pass_on(p, s):
        right1, left1, _, _ = roles[p]
        for side, origin in ((0, left1), (1, right1)):
            arrived(along1[p][s][side], block_kib)
            forward(p, origin, column(p, s), axes[p][0], roles[p][side], side, fwd1[p][s])
            finished(p, origin, column(p, s))

    for s in range(3):
        for p in range(2):
            pass_on(p, s)
    for s in range(3):
        for p in range(2):
            arrived(fwd1[p][s], block_kib)
            finished(p, roles[p][3], column(p, s))
    for n, role in ((1, 1), (2, 0), (0, 3)):
        for p in range(2):
            arrived(along1[p][3][n], block_kib)
            finished(p, roles[p][role], column(p, 3))
    arrived(to_pair, size(o_w.at[0]))
    all_sent()
    assert groups[0] <= SEMS and groups[1] <= LOCAL_SEMS, (groups, sent)


def write_out(*refs):
    sems = refs[12]
    copies = [pltpu.make_async_copy(refs[k], refs[k + 6], sems.at[k]) for k in (5, 0, 1, 2, 3, 4)]
    for copy in copies:
        copy.start()
    for copy in copies:
        copy.wait()


def body(partials, master, m_codes, v_codes, m_scales, v_scales):
    any_spec = pl.BlockSpec(memory_space=pl.ANY)
    vmem = pltpu.VMEM
    small = [pltpu.with_memory_space_constraint(a, pltpu.HBM) for a in (master, m_codes, v_codes, m_scales, v_scales)]
    results = pl.pallas_call(
        kernel,
        out_shape=(
            jax.ShapeDtypeStruct(master.shape, F32),
            jax.ShapeDtypeStruct(master.shape, BF16),
            jax.ShapeDtypeStruct(master.shape, BF16),
            jax.ShapeDtypeStruct(m_scales.shape, F32),
            jax.ShapeDtypeStruct(m_scales.shape, F32),
            jax.ShapeDtypeStruct((2, V, D), BF16),
        ),
        in_specs=[pl.BlockSpec(memory_space=pltpu.HBM)] * 6,
        out_specs=(pl.BlockSpec(memory_space=pltpu.VMEM),) * 6,
        scratch_shapes=[
            vmem((2, 3, V, WIDE), BF16),
            vmem((2, 3, V, WIDE), BF16),
            vmem((2, 2, 2, V, WIDE // 2), BF16),
            vmem((2, 2, V, WIDE), F32),
            vmem((2, 2, V, WIDE), F32),
            vmem((2, V, WIDE), F32),
            vmem((2, 3, V, SUB), F32),
            vmem((2, V, SUB), F32),
            vmem((2, 7, TILE, SUB), F32),
            vmem((2, TILE, SUB), F32),
            vmem((16, 8, 128), F32),
            vmem((16, 8, 128), F32),
            vmem((8, 2, 2, SUB), F32),
            vmem((8, 2, 2, SUB), BF16),
            vmem((8, 2, 2, SUB), BF16),
            vmem((8, 4, 128), F32),
            vmem((2, 4, 128), F32),
            vmem((2, TILE, SUB), F32),
            vmem((2, TILE, SUB), F32),
            vmem((2, TILE, SUB), F32),
            vmem((8, 2, 2, SUB), F32),
            vmem((8, 2, 2, SUB), F32),
            vmem((4, 8, 2, 2, SUB), F32),
            vmem((2, 2, D), F32),
            vmem((2, 2, D), BF16),
            vmem((2, 2, D), BF16),
            vmem((2, 2, 4), F32),
            vmem((2, 2, 4), F32),
            vmem((LIMIT_KIB, 2, 128), F32),
            pltpu.SemaphoreType.DMA((1,)),
            pltpu.SemaphoreType.DMA((SEMS,)),
            pltpu.SemaphoreType.DMA((LOCAL_SEMS,)),
        ],
        compiler_params=pltpu.CompilerParams(
            collective_id=0, has_side_effects=True, vmem_limit_bytes=48 * 1024 * 1024
        ),
        name="step",
    )(partials, *small)
    return pl.pallas_call(
        write_out,
        out_shape=tuple(jax.ShapeDtypeStruct(a.shape, a.dtype) for a in results),
        in_specs=[any_spec] * 6,
        out_specs=(any_spec,) * 6,
        scratch_shapes=[pltpu.SemaphoreType.DMA((6,))],
        compiler_params=pltpu.CompilerParams(vmem_limit_bytes=1024 * 1024),
        name="write_out",
    )(*results)


def solution(mesh):
    finer = Mesh(mesh.devices.reshape(NZ, NX, NC, NY), ("z", "x", "c", "y"))
    rows = P(None, ("z", "x", "c"), None)
    return jax.shard_map(
        body,
        mesh=finer,
        in_specs=(P("y", ("z", "x", "c"), None, None, None),) + (rows,) * 5,
        out_specs=(rows,) * 5 + (P(),),
        check_vma=False,
    )
```

time: 89.3 us -> 80.9 us (0.906)
  Pallas kernels: 88.6 us -> 80.1 us
    pallas_call x1, Pallas kernels: 86.4 us -> 78 us  [body(): pl.pallas_call(kernel, out_shape=(jax.ShapeDtypeStruct(master.shape, F32)...]
where the time goes in v3:
time: 80.9 us; the launch traced here: 80.8 us
  Pallas kernels  80.1 us (99%)
    pallas_call x1, Pallas kernels, body(): pl.pallas_call(kernel, out_shape=(jax.ShapeDtypeStruct(master.shape, F32)...  78 us
    pallas_call x1, Pallas kernels, body(): pl.pallas_call(write_out, out_shape=tuple((jax.ShapeDtypeStruct(a.shape,...  2.13 us

profile of v3, /device:TPU:1, one launch (start us, length us, event | category | flops | bytes accessed | tf_op | source)
XLA Modules:
  0.0 80.8 jit_solution(13069263769118923164)
XLA Ops:
  0.6 78.0 %step.1 = (f32[2,2,8192]{2,1,0:T(2,128)S(1)}, bf16[2,2,8192]{2,1,0:T(2,128)(2,1)S(1)}, bf16[2,2,8192]{2,1,0:T(2,128)(2,1)S(1)}, f32[2,2,4]{2,1,0:T(2,128)S(1)}, ...) custom-call(bf16[1,1,2,128,8192]{4,3,2,1,0:T(8,128)(2,1)} %part_in.1, f32[2,2,8192]{2,1,0:T(2,128)} %master_in.1, ...), custom_call_target="tpu_custom_call" | custom-call | tf_op jit(solution)/shard_map/step/pallas_call | solution.py:401
  78.7 2.1 %write_out.1 = (f32[2,2,8192]{2,1,0:T(2,128)}, bf16[2,2,8192]{2,1,0:T(2,128)(2,1)}, bf16[2,2,8192]{2,1,0:T(2,128)(2,1)}, f32[2,2,4]{2,1,0:T(2,128)}, f32[2,2,4]{2,1,0:T(2,128)}, /*index=5*/bf16[2,128,8192]{2,1,0:T(8,128)(2,1)}) custom-call(f32[2,2,8192]{2,1,0:T(2,128)S(1)} %get-tuple-element.12.refs_0_, bf16[2,2,8192]{2,1,0:T(2,128)(2,1)S(1)} %get-tuple-element.13.refs_1_, ...), custom_call_target="tpu_custom_call" | custom-call | tf_op jit(solution)/shard_map/write_out/pallas_call | solution.py:452

commit v4 on v3

--- a/solution.py
+++ b/solution.py
@@ -47,7 +47,7 @@
     o_master, o_mc, o_vc, o_ms, o_vs, o_w,
     own, par, rcv1, snd, rcv2, s_buf, p2f, t_buf, z_buf, g_buf,
     nzc, nxy,
-    e_master, e_mc, e_vc, e_s, sc_stage, mt, vt, wt,
+    e_master, e_mc, e_vc, e_s, sc_stage, tile, st, g_col,
     q_s, q_r, g_full,
     l_master, l_mc, l_vc, l_ms, l_vs, bytes_ref,
     ssem, rsem, lsem,
@@ -120,37 +120,6 @@
         pl.semaphore_signal(barrier, inc=1, device_id=dev, device_id_type=MESH)
     pl.semaphore_wait(barrier, len(greeted))
 
-    raw = [[group() for _ in range(2)] for _ in range(2)]
-    for q in range(2):
-        m = lax.rem(c + q, 2)
-        for p in range(2):
-            axis = axes[p][0]
-            for h in range(2):
-                cols = pl.ds(col(p * HALF + roles[p][3] * WIDE + h * (WIDE // 2), WIDE // 2), WIDE // 2)
-                send(part_in.at[0, 0, m, :, cols], rcv1.at[p, h, q], raw[p][h], **{axis: roles[p][h], "c": m})
-    pair = [[group() for _ in range(3)] for _ in range(2)]
-    for role in range(3):
-        for p in range(2):
-            cols = pl.ds(col(p * HALF + roles[p][role] * WIDE, WIDE), WIDE)
-            send(part_in.at[0, 0, other, :, cols], par.at[p, role], pair[p][role], c=other)
-
-    from_side = [[group() for _ in range(2)] for _ in range(2)]
-    for p in range(2):
-        axis = axes[p][0]
-        for side in range(2):
-            own_loads[p][side].wait()
-            arrived(pair[p][side], size(par.at[p, side]))
-            lo = (1 - side) * (WIDE // 2)
-
-            @pl.loop(0, V // TILE)
-            def _(t):
-                rows = pl.ds(pl.multiple_of(t * TILE, TILE), TILE)
-                cc = pl.ds(lo, WIDE // 2)
-                snd[p, side, rows, cc] = own[p, side, rows, cc].astype(F32) + par[p, side, rows, cc].astype(F32)
-
-            cc = pl.ds(lo, WIDE // 2)
-            send(snd.at[p, side, :, cc], rcv2.at[p, side, :, cc], from_side[p][side], **{axis: roles[p][side]})
-
     state = group()
     tile_cols = [
         lambda kx: col(kx * WIDE + y * SUB, SUB),
@@ -162,6 +131,20 @@
             own_state.append(local(src.at[c, :, pl.ds(tile_cols[p](x), SUB)], dst.at[own_k, p]))
             for k, dev in xc_peers:
                 send(src.at[dev["c"], :, pl.ds(tile_cols[p](dev["x"]), SUB)], dst.at[own_k, p], state, **dev)
+    raw = [[group() for _ in range(2)] for _ in range(2)]
+    for q in range(2):
+        m = lax.rem(c + q, 2)
+        for p in range(2):
+            axis = axes[p][0]
+            for h in range(2):
+                cols = pl.ds(col(p * HALF + roles[p][3] * WIDE + h * (WIDE // 2), WIDE // 2), WIDE // 2)
+                send(part_in.at[0, 0, m, :, cols], rcv1.at[p, h, q], raw[p][h], **{axis: roles[p][h], "c": m})
+    pair = [[group() for _ in range(3)] for _ in range(2)]
+    for role in range(3):
+        for p in range(2):
+            cols = pl.ds(col(p * HALF + roles[p][role] * WIDE, WIDE), WIDE)
+            send(part_in.at[0, 0, other, :, cols], par.at[p, role], pair[p][role], c=other)
+
     for load in state_loads:
         load.wait()
     sc_stage[...] = jnp.zeros_like(sc_stage)
@@ -172,20 +155,19 @@
     for k, dev in xc_peers:
         send(sc_stage.at[dev["c"]], e_s.at[own_k], state, **dev)
 
+    from_side = [[group() for _ in range(2)] for _ in range(2)]
     for p in range(2):
         axis = axes[p][0]
         for side in range(2):
-            h = side
-            lo = h * (WIDE // 2)
-            arrived(raw[p][h], size(rcv1.at[p, h]))
+            own_loads[p][side].wait()
+            arrived(pair[p][side], size(par.at[p, side]))
+            lo = (1 - side) * (WIDE // 2)
 
             @pl.loop(0, V // TILE)
             def _(t):
                 rows = pl.ds(pl.multiple_of(t * TILE, TILE), TILE)
                 cc = pl.ds(lo, WIDE // 2)
-                near = own[p, side, rows, cc].astype(F32) + par[p, side, rows, cc].astype(F32)
-                far = rcv1[p, h, 0, rows, :].astype(F32) + rcv1[p, h, 1, rows, :].astype(F32)
-                snd[p, side, rows, cc] = near + far
+                snd[p, side, rows, cc] = own[p, side, rows, cc].astype(F32) + par[p, side, rows, cc].astype(F32)
 
             cc = pl.ds(lo, WIDE // 2)
             send(snd.at[p, side, :, cc], rcv2.at[p, side, :, cc], from_side[p][side], **{axis: roles[p][side]})
@@ -200,28 +182,81 @@
         for p in range(2):
             scale = jnp.sum(jnp.where(lane == blocks[p], e, 0.0), axis=1, keepdims=True)
             rows = pl.ds(2 * k, 2)
-            mt[p, rows, :] = e_mc[k, p].astype(F32) * scale[0:2]
-            vt[p, rows, :] = e_vc[k, p].astype(F32) * scale[2:4]
-            wt[p, rows, :] = e_master[k, p]
+            tile[0, p, rows, :] = e_mc[k, p].astype(F32) * scale[0:2]
+            tile[1, p, rows, :] = e_vc[k, p].astype(F32) * scale[2:4]
+            tile[2, p, rows, :] = e_master[k, p]
+    my_rows = pl.ds(pl.multiple_of(z * TILE, TILE), TILE)
+    z_next, z_last = {"z": mod(z + 1, 8)}, {"z": mod(z - 1, 8)}
+    z_rows = lambda d: pl.ds(pl.multiple_of(mod(z + d, 8) * TILE, TILE), TILE)
+    column_state = [group() for _ in range(4)]
+    send(tile, st.at[:, :, my_rows, :], column_state[0], **z_next)
+    send(tile, st.at[:, :, my_rows, :], column_state[0], **z_last)
+
+    def pass_state(n):
+        arrived(column_state[n - 1], 2 * 96)
+        for d, dev, p in ((-n, z_next, 0), (n, z_last, 1)):
+            ref = st.at[:, :, z_rows(d), :] if n < 3 else st.at[:, p, z_rows(d), :]
+            send(ref, ref, column_state[n], **dev)
+
+    for n in range(3):
+        for p in range(2):
+            st[n, p, my_rows, :] = tile[n, p]
+
+    half_subs = []
+    for p in range(2):
+        i2 = axes[p][3]
+        half_subs.append([
+            tuple(2 * h + lax.rem(i2 + i2 // 2 + h + 1 - n, 2) for h in range(2)) for n in range(2)
+        ])
+    relay = [[[group() for _ in range(2)] for _ in range(2)] for _ in range(2)]
+    for n in range(2):
+        for p in range(2):
+            axis = axes[p][0]
+            for side in range(2):
+                sub = half_subs[p][n][side]
+                if n == 0:
+                    arrived(raw[p][side], size(rcv1.at[p, side]))
+                cc = pl.ds(col(sub * SUB, SUB), SUB)
+                cr = pl.ds(col((sub - 2 * side) * SUB, SUB), SUB)
+
+                @pl.loop(0, V // TILE)
+                def _(t):
+                    rows = pl.ds(pl.multiple_of(t * TILE, TILE), TILE)
+                    near = own[p, side, rows, cc].astype(F32) + par[p, side, rows, cc].astype(F32)
+                    far = rcv1[p, side, 0, rows, cr].astype(F32) + rcv1[p, side, 1, rows, cr].astype(F32)
+                    snd[p, side, rows, cc] = near + far
+
+                send(snd.at[p, side, :, cc], rcv2.at[p, side, :, cc], relay[p][side][n], **{axis: roles[p][side]})
+    pass_state(1)
 
     second = [group() for _ in range(2)]
-    for p in range(2):
-        axis2, r2 = axes[p][2], roles2[p]
-        own_loads[p][2].wait()
-        arrived(pair[p][2], size(par.at[p, 2]))
-        for side in range(2):
-            arrived(from_side[p][side], size(rcv2.at[p, side]))
-        for n in (3, 0, 1, 2):
-            cols = pl.ds(col(r2[n] * SUB, SUB), SUB)
-
-            @pl.loop(0, V // TILE)
-            def _(t):
-                rows = pl.ds(pl.multiple_of(t * TILE, TILE), TILE)
-                near = own[p, 2, rows, cols].astype(F32) + par[p, 2, rows, cols].astype(F32)
-                s_buf[p, rows, cols] = near + rcv2[p, 0, rows, cols] + rcv2[p, 1, rows, cols]
-
-            if n != 2:
-                send(s_buf.at[p, :, cols], p2f.at[p, n if n < 2 else 2], second[p], **{axis2: r2[n]})
+    for n in range(2):
+        for p in range(2):
+            axis2, i2 = axes[p][2], axes[p][3]
+            if n == 0:
+                own_loads[p][2].wait()
+                arrived(pair[p][2], size(par.at[p, 2]))
+                for side in range(2):
+                    arrived(from_side[p][side], size(rcv2.at[p, side]) // 2)
+            for h in range(2):
+                arrived(relay[p][h][n], size(rcv2.at[p, h]) // 4)
+                cols = pl.ds(col(half_subs[p][n][h] * SUB, SUB), SUB)
+
+                @pl.loop(0, V // TILE)
+                def _(t):
+                    rows = pl.ds(pl.multiple_of(t * TILE, TILE), TILE)
+                    near = own[p, 2, rows, cols].astype(F32) + par[p, 2, rows, cols].astype(F32)
+                    s_buf[p, rows, cols] = near + rcv2[p, 0, rows, cols] + rcv2[p, 1, rows, cols]
+
+            opp2 = roles2[p][3]
+            if n == 0:
+                targets = ((opp2, 0), (i2 + 1 - 2 * lax.rem(i2, 2), 1))
+            else:
+                targets = ((opp2 + 1 - 2 * lax.rem(opp2, 2), 2),)
+            for target, slot in targets:
+                cols = pl.ds(col(target * SUB, SUB), SUB)
+                send(s_buf.at[p, :, cols], p2f.at[p, slot], second[p], **{axis2: target})
+        pass_state(2 + n)
 
     third = [group() for _ in range(2)]
     for p in range(2):
@@ -239,7 +274,6 @@
             rows = pl.ds(pl.multiple_of(zd * TILE, TILE), TILE)
             send(t_buf.at[p, rows, :], z_buf.at[p, d - 1], third[p], z=zd)
 
-    my_rows = pl.ds(pl.multiple_of(z * TILE, TILE), TILE)
     square = jnp.zeros((8, 128), F32)
     for p in range(2):
         arrived(third[p], size(z_buf.at[p]))
@@ -247,15 +281,18 @@
         for d in range(7):
             g = g + z_buf[p, d]
         g_buf[p] = g
+        g_col[p, my_rows, :] = g
         sq = g * g
         for i in range(2):
             for j in range(2):
                 square = square + sq[8 * i:8 * i + 8, 128 * j:128 * j + 128]
-    norm_zc, norm_xy, q1, q2 = (group() for _ in range(4))
+    norm_zc, norm_xy, q1, q2, column_g = (group() for _ in range(5))
     slot = 2 * z + c
     nzc[slot] = square
     for dev in zc_peers:
         send(nzc.at[slot], nzc.at[slot], norm_zc, **dev)
+    for d in (4, 3, 5, 2, 6, 1, 7):
+        send(g_buf, g_col.at[:, my_rows, :], column_g, z=mod(z + d, 8))
 
     for p in range(2):
         for k in range(8):
@@ -281,15 +318,42 @@
     clip = 1.0 / jnp.maximum(jnp.sqrt(total), 1.0)
 
     block_of = lambda p, i, j: pl.ds(col(p * HALF + i * WIDE + j * SUB, SUB), SUB)
+    to_pair = group()
+    rows_half = (pl.ds(0, V // 2), pl.ds(V // 2, V // 2))
+    block_kib = V * SUB * 2 // 1024
+
+    def finished(p, i, j):
+        ref = o_w.at[c, :, block_of(p, i, j)]
+        send(ref, ref, to_pair, c=other)
+
+    def spread(p, i, j, axis, targets):
+        ref = o_w.at[c, :, block_of(p, i, j)]
+        ks = [group() for _ in targets]
+        for k, target in zip(ks, targets):
+            send(ref, ref, k, **{axis: target})
+        return ks
+
+    def forward(p, i, j, axis, target, h, k):
+        ref = o_w.at[c, rows_half[h], block_of(p, i, j)]
+        send(ref, ref, k, **{axis: target})
+
+    arrived(column_state[3], 96)
+    arrived(column_g, 7 * 32)
+    along2, along1 = [None] * 2, [[None] * 4 for _ in range(2)]
     for p in range(2):
-        i1, i2 = axes[p][1], axes[p][3]
-        _, _, fresh = adam(mt[p], vt[p], clip * g_buf[p], wt[p])
-        o_w[c, my_rows, block_of(p, i1, i2)] = fresh.astype(BF16)
-    ag1 = [group() for _ in range(2)]
-    for d in (4, 3, 5, 2, 6, 1, 7):
-        for p in range(2):
-            ref = o_w.at[c, my_rows, block_of(p, axes[p][1], axes[p][3])]
-            send(ref, ref, ag1[p], z=mod(z + d, 8))
+        a1, i1, a2, i2 = axes[p]
+        cols = block_of(p, i1, i2)
+
+        @pl.loop(0, V // TILE)
+        def _(t):
+            rows = pl.ds(pl.multiple_of(t * TILE, TILE), TILE)
+            _, _, fresh = adam(st[0, p, rows], st[1, p, rows], clip * g_col[p, rows], st[2, p, rows])
+            o_w[c, rows, cols] = fresh.astype(BF16)
+
+        right2, left2, _, opp2 = roles2[p]
+        along2[p] = spread(p, i1, i2, a2, (opp2, right2, left2))
+        along1[p][0] = spread(p, i1, i2, a1, roles[p][:2])
+        finished(p, i1, i2)
 
     arrived(q2, 3 * 32)
     lane4 = lax.broadcasted_iota(jnp.int32, (2, 4), 1)
@@ -318,34 +382,6 @@
             tops_v = jnp.where(lane4 == b, v_top, tops_v)
         o_ms[m] = tops_m
         o_vs[m] = tops_v
-
-    to_pair = group()
-    rows_half = (pl.ds(0, V // 2), pl.ds(V // 2, V // 2))
-    block_kib = V * SUB * 2 // 1024
-
-    def finished(p, i, j):
-        ref = o_w.at[c, :, block_of(p, i, j)]
-        send(ref, ref, to_pair, c=other)
-
-    def spread(p, i, j, axis, targets):
-        ref = o_w.at[c, :, block_of(p, i, j)]
-        ks = [group() for _ in targets]
-        for k, target in zip(ks, targets):
-            send(ref, ref, k, **{axis: target})
-        return ks
-
-    def forward(p, i, j, axis, target, h, k):
-        ref = o_w.at[c, rows_half[h], block_of(p, i, j)]
-        send(ref, ref, k, **{axis: target})
-
-    along2, along1 = [None] * 2, [[None] * 4 for _ in range(2)]
-    for p in range(2):
-        a1, i1, a2, i2 = axes[p]
-        arrived(ag1[p], 7 * TILE * SUB * 2 // 1024)
-        right2, left2, _, opp2 = roles2[p]
-        along2[p] = spread(p, i1, i2, a2, (opp2, right2, left2))
-        along1[p][0] = spread(p, i1, i2, a1, roles[p][:2])
-        finished(p, i1, i2)
     for n, s in ((1, 1), (2, 2), (0, 3)):
         for p in range(2):
             a1, i1, a2, i2 = axes[p]
@@ -428,9 +464,9 @@
             vmem((8, 2, 2, SUB), BF16),
             vmem((8, 4, 128), F32),
             vmem((2, 4, 128), F32),
-            vmem((2, TILE, SUB), F32),
-            vmem((2, TILE, SUB), F32),
-            vmem((2, TILE, SUB), F32),
+            vmem((3, 2, TILE, SUB), F32),
+            vmem((3, 2, V, SUB), F32),
+            vmem((2, V, SUB), F32),
             vmem((8, 2, 2, SUB), F32),
             vmem((8, 2, 2, SUB), F32),
             vmem((4, 8, 2, 2, SUB), F32),

time: 80.9 us -> 75.8 us (0.937)
  Pallas kernels: 80.1 us -> 75 us
    pallas_call x1, Pallas kernels: 78 us -> 72.9 us  [body(): pl.pallas_call(kernel, out_shape=(jax.ShapeDtypeStruct(master.shape, F32)...]
where the time goes in v4:
time: 75.8 us; the launch traced here: 75.7 us
  Pallas kernels  75 us (99%)
    pallas_call x1, Pallas kernels, body(): pl.pallas_call(kernel, out_shape=(jax.ShapeDtypeStruct(master.shape, F32)...  72.9 us
    pallas_call x1, Pallas kernels, body(): pl.pallas_call(write_out, out_shape=tuple((jax.ShapeDtypeStruct(a.shape,...  2.13 us

profile of v4, /device:TPU:1, one launch (start us, length us, event | category | flops | bytes accessed | tf_op | source)
XLA Modules:
  0.0 75.7 jit_solution(14499963120578140)
XLA Ops:
  0.6 72.9 %step.1 = (f32[2,2,8192]{2,1,0:T(2,128)S(1)}, bf16[2,2,8192]{2,1,0:T(2,128)(2,1)S(1)}, bf16[2,2,8192]{2,1,0:T(2,128)(2,1)S(1)}, f32[2,2,4]{2,1,0:T(2,128)S(1)}, ...) custom-call(bf16[1,1,2,128,8192]{4,3,2,1,0:T(8,128)(2,1)} %part_in.1, f32[2,2,8192]{2,1,0:T(2,128)} %master_in.1, ...), custom_call_target="tpu_custom_call" | custom-call | tf_op jit(solution)/shard_map/step/pallas_call | solution.py:437
  73.5 2.1 %write_out.1 = (f32[2,2,8192]{2,1,0:T(2,128)}, bf16[2,2,8192]{2,1,0:T(2,128)(2,1)}, bf16[2,2,8192]{2,1,0:T(2,128)(2,1)}, f32[2,2,4]{2,1,0:T(2,128)}, f32[2,2,4]{2,1,0:T(2,128)}, /*index=5*/bf16[2,128,8192]{2,1,0:T(8,128)(2,1)}) custom-call(f32[2,2,8192]{2,1,0:T(2,128)S(1)} %get-tuple-element.12.refs_0_, bf16[2,2,8192]{2,1,0:T(2,128)(2,1)S(1)} %get-tuple-element.13.refs_1_, ...), custom_call_target="tpu_custom_call" | custom-call | tf_op jit(solution)/shard_map/write_out/pallas_call | solution.py:488

commit v5 on v4

--- a/solution.py
+++ b/solution.py
@@ -57,7 +57,7 @@
     groups, sent = [0, 0], [0]
 
     def size(ref):
-        return math.prod(ref.shape) * ref.dtype.itemsize // 1024
+        return math.prod(ref.shape) * ref.dtype.itemsize / 1024
 
     def group():
         groups[0] += 1
@@ -71,12 +71,15 @@
         ).start()
 
     def arrived(k, kib):
-        ref = bytes_ref.at[pl.ds(0, kib)]
+        ref = bytes_ref.at[pl.ds(0, int(2 * kib))]
         pltpu.make_async_copy(ref, ref, rsem.at[k]).wait()
+
+    def arrived_words(k, slots):
+        arrived(k, 15 * size(slots.at[0]))
 
     def all_sent():
         assert sent[0] <= LIMIT_KIB
-        ref = bytes_ref.at[pl.ds(0, sent[0])]
+        ref = bytes_ref.at[pl.ds(0, int(2 * sent[0]))]
         pltpu.make_async_copy(ref, ref, ssem.at[0]).wait()
 
 
@@ -120,6 +123,20 @@
         pl.semaphore_signal(barrier, inc=1, device_id=dev, device_id_type=MESH)
     pl.semaphore_wait(barrier, len(greeted))
 
+    raw = [[group() for _ in range(2)] for _ in range(2)]
+    for q in range(2):
+        m = lax.rem(c + q, 2)
+        for p in range(2):
+            axis = axes[p][0]
+            for h in range(2):
+                cols = pl.ds(col(p * HALF + roles[p][3] * WIDE + h * (WIDE // 2), WIDE // 2), WIDE // 2)
+                send(part_in.at[0, 0, m, :, cols], rcv1.at[p, h, q], raw[p][h], **{axis: roles[p][h], "c": m})
+    pair = [[group() for _ in range(3)] for _ in range(2)]
+    for role in range(3):
+        for p in range(2):
+            cols = pl.ds(col(p * HALF + roles[p][role] * WIDE, WIDE), WIDE)
+            send(part_in.at[0, 0, other, :, cols], par.at[p, role], pair[p][role], c=other)
+
     state = group()
     tile_cols = [
         lambda kx: col(kx * WIDE + y * SUB, SUB),
@@ -131,20 +148,6 @@
             own_state.append(local(src.at[c, :, pl.ds(tile_cols[p](x), SUB)], dst.at[own_k, p]))
             for k, dev in xc_peers:
                 send(src.at[dev["c"], :, pl.ds(tile_cols[p](dev["x"]), SUB)], dst.at[own_k, p], state, **dev)
-    raw = [[group() for _ in range(2)] for _ in range(2)]
-    for q in range(2):
-        m = lax.rem(c + q, 2)
-        for p in range(2):
-            axis = axes[p][0]
-            for h in range(2):
-                cols = pl.ds(col(p * HALF + roles[p][3] * WIDE + h * (WIDE // 2), WIDE // 2), WIDE // 2)
-                send(part_in.at[0, 0, m, :, cols], rcv1.at[p, h, q], raw[p][h], **{axis: roles[p][h], "c": m})
-    pair = [[group() for _ in range(3)] for _ in range(2)]
-    for role in range(3):
-        for p in range(2):
-            cols = pl.ds(col(p * HALF + roles[p][role] * WIDE, WIDE), WIDE)
-            send(part_in.at[0, 0, other, :, cols], par.at[p, role], pair[p][role], c=other)
-
     for load in state_loads:
         load.wait()
     sc_stage[...] = jnp.zeros_like(sc_stage)
@@ -206,18 +209,19 @@
     for p in range(2):
         i2 = axes[p][3]
         half_subs.append([
-            tuple(2 * h + lax.rem(i2 + i2 // 2 + h + 1 - n, 2) for h in range(2)) for n in range(2)
+            tuple(2 * h + lax.rem(i2 + i2 // 2 + h + 1 - min(n, 1), 2) for h in range(2)) for n in range(3)
         ])
-    relay = [[[group() for _ in range(2)] for _ in range(2)] for _ in range(2)]
-    for n in range(2):
+    starts, widths = (0, 0, SUB // 2), (SUB, SUB // 2, SUB // 2)
+    relay = [[[group() for _ in range(3)] for _ in range(2)] for _ in range(2)]
+    for n in range(3):
         for p in range(2):
             axis = axes[p][0]
             for side in range(2):
                 sub = half_subs[p][n][side]
                 if n == 0:
                     arrived(raw[p][side], size(rcv1.at[p, side]))
-                cc = pl.ds(col(sub * SUB, SUB), SUB)
-                cr = pl.ds(col((sub - 2 * side) * SUB, SUB), SUB)
+                cc = pl.ds(col(sub * SUB + starts[n], SUB // 2), widths[n])
+                cr = pl.ds(col((sub - 2 * side) * SUB + starts[n], SUB // 2), widths[n])
 
                 @pl.loop(0, V // TILE)
                 def _(t):
@@ -229,8 +233,8 @@
                 send(snd.at[p, side, :, cc], rcv2.at[p, side, :, cc], relay[p][side][n], **{axis: roles[p][side]})
     pass_state(1)
 
-    second = [group() for _ in range(2)]
-    for n in range(2):
+    second = [[group() for _ in range(3)] for _ in range(2)]
+    for n in range(3):
         for p in range(2):
             axis2, i2 = axes[p][2], axes[p][3]
             if n == 0:
@@ -239,8 +243,8 @@
                 for side in range(2):
                     arrived(from_side[p][side], size(rcv2.at[p, side]) // 2)
             for h in range(2):
-                arrived(relay[p][h][n], size(rcv2.at[p, h]) // 4)
-                cols = pl.ds(col(half_subs[p][n][h] * SUB, SUB), SUB)
+                arrived(relay[p][h][n], V * widths[n] * 4 / 1024)
+                cols = pl.ds(col(half_subs[p][n][h] * SUB + starts[n], SUB // 2), widths[n])
 
                 @pl.loop(0, V // TILE)
                 def _(t):
@@ -254,41 +258,48 @@
             else:
                 targets = ((opp2 + 1 - 2 * lax.rem(opp2, 2), 2),)
             for target, slot in targets:
-                cols = pl.ds(col(target * SUB, SUB), SUB)
-                send(s_buf.at[p, :, cols], p2f.at[p, slot], second[p], **{axis2: target})
-        pass_state(2 + n)
-
-    third = [group() for _ in range(2)]
-    for p in range(2):
-        r2 = roles2[p]
-        arrived(second[p], size(p2f.at[p]))
-        cols = pl.ds(col(r2[2] * SUB, SUB), SUB)
-
-        @pl.loop(0, V // TILE)
-        def _(t):
-            rows = pl.ds(pl.multiple_of(t * TILE, TILE), TILE)
-            t_buf[p, rows, :] = s_buf[p, rows, cols] + p2f[p, 0, rows] + (p2f[p, 1, rows] + p2f[p, 2, rows])
-
-        for d in (4, 3, 5, 2, 6, 1, 7):
-            zd = mod(z + d, 8)
-            rows = pl.ds(pl.multiple_of(zd * TILE, TILE), TILE)
-            send(t_buf.at[p, rows, :], z_buf.at[p, d - 1], third[p], z=zd)
+                cols = pl.ds(col(target * SUB + starts[n], SUB // 2), widths[n])
+                send(s_buf.at[p, :, cols], p2f.at[p, slot, :, starts[n]:starts[n] + widths[n]], second[p][n],
+                     **{axis2: target})
+        if n < 2:
+            pass_state(2 + n)
+
+    third = [[group() for _ in range(2)] for _ in range(2)]
+    for q in range(2):
+        for p in range(2):
+            i2 = axes[p][3]
+            if q == 0:
+                arrived(second[p][0], 2 * V * SUB * 4 / 1024)
+            arrived(second[p][1 + q], V * SUB * 2 / 1024)
+            cols = pl.ds(col(i2 * SUB + q * (SUB // 2), SUB // 2), SUB // 2)
+            cq = pl.ds(q * (SUB // 2), SUB // 2)
+
+            @pl.loop(0, V // TILE)
+            def _(t):
+                rows = pl.ds(pl.multiple_of(t * TILE, TILE), TILE)
+                t_buf[p, q, rows, :] = s_buf[p, rows, cols] + p2f[p, 0, rows, cq] + (
+                    p2f[p, 1, rows, cq] + p2f[p, 2, rows, cq])
+
+            for d in (4, 3, 5, 2, 6, 1, 7):
+                zd = mod(z + d, 8)
+                rows = pl.ds(pl.multiple_of(zd * TILE, TILE), TILE)
+                send(t_buf.at[p, q, rows, :], z_buf.at[p, q, d - 1], third[p][q], z=zd)
 
     square = jnp.zeros((8, 128), F32)
-    for p in range(2):
-        arrived(third[p], size(z_buf.at[p]))
-        g = t_buf[p, my_rows, :]
-        for d in range(7):
-            g = g + z_buf[p, d]
-        g_buf[p] = g
-        g_col[p, my_rows, :] = g
-        sq = g * g
-        for i in range(2):
-            for j in range(2):
-                square = square + sq[8 * i:8 * i + 8, 128 * j:128 * j + 128]
+    for q in range(2):
+        for p in range(2):
+            arrived(third[p][q], size(z_buf.at[p, q]))
+            g = t_buf[p, q, my_rows, :]
+            for d in range(7):
+                g = g + z_buf[p, q, d]
+            cq = slice(q * (SUB // 2), (q + 1) * (SUB // 2))
+            g_buf[p, :, cq] = g
+            g_col[p, my_rows, cq] = g
+            sq = g * g
+            square = square + sq[0:8] + sq[8:16]
     norm_zc, norm_xy, q1, q2, column_g = (group() for _ in range(5))
     slot = 2 * z + c
-    nzc[slot] = square
+    nzc[slot] = jnp.sum(square, axis=0, keepdims=True)
     for dev in zc_peers:
         send(nzc.at[slot], nzc.at[slot], norm_zc, **dev)
     for d in (4, 3, 5, 2, 6, 1, 7):
@@ -301,7 +312,7 @@
         send(q_s.at[k], q_r.at[own_k], q1, **dev)
     q_r[own_k] = q_s[own_k]
 
-    arrived(norm_zc, 15 * 4)
+    arrived_words(norm_zc, nzc)
     slot = 4 * x + y
     nxy[slot] = functools.reduce(lambda a, b: a + b, [nzc[k] for k in range(16)])
     for dev in xy_peers:
@@ -312,9 +323,9 @@
         send(q_r, g_full.at[y], q2, y=mod(y + d, 4))
     g_full[y] = q_r[...]
 
-    arrived(norm_xy, 15 * 4)
+    arrived_words(norm_xy, nxy)
     total = functools.reduce(lambda a, b: a + b, [nxy[k] for k in range(16)])
-    total = jnp.sum(jnp.sum(total, axis=1, keepdims=True), axis=0, keepdims=True)
+    total = jnp.sum(total, axis=1, keepdims=True)
     clip = 1.0 / jnp.maximum(jnp.sqrt(total), 1.0)
 
     block_of = lambda p, i, j: pl.ds(col(p * HALF + i * WIDE + j * SUB, SUB), SUB)
@@ -351,9 +362,31 @@
             o_w[c, rows, cols] = fresh.astype(BF16)
 
         right2, left2, _, opp2 = roles2[p]
-        along2[p] = spread(p, i1, i2, a2, (opp2, right2, left2))
+        along2[p] = spread(p, i1, i2, a2, (right2, left2, opp2))
         along1[p][0] = spread(p, i1, i2, a1, roles[p][:2])
         finished(p, i1, i2)
+
+    for n, s in ((1, 1), (0, 2), (2, 3)):
+        for p in range(2):
+            a1, i1, a2, i2 = axes[p]
+            right2, left2, _, opp2 = roles2[p]
+            origin = (left2, right2, opp2)[n]
+            arrived(along2[p][n], block_kib)
+            along1[p][s] = spread(p, i1, origin, a1, roles[p][:2])
+            finished(p, i1, origin)
+
+    fwd1 = [[group() for _ in range(4)] for _ in range(2)]
+
+    def column(p, s):
+        right2, left2, _, opp2 = roles2[p]
+        return (axes[p][3], right2, left2, opp2)[s]
+
+    def pass_on(p, s):
+        right1, left1, _, _ = roles[p]
+        for side, origin in ((0, left1), (1, right1)):
+            arrived(along1[p][s][side], block_kib)
+            forward(p, origin, column(p, s), axes[p][0], roles[p][side], side, fwd1[p][s])
+            finished(p, origin, column(p, s))
 
     arrived(q2, 3 * 32)
     lane4 = lax.broadcasted_iota(jnp.int32, (2, 4), 1)
@@ -382,40 +415,13 @@
             tops_v = jnp.where(lane4 == b, v_top, tops_v)
         o_ms[m] = tops_m
         o_vs[m] = tops_v
-    for n, s in ((1, 1), (2, 2), (0, 3)):
-        for p in range(2):
-            a1, i1, a2, i2 = axes[p]
-            right2, left2, _, opp2 = roles2[p]
-            origin = (opp2, left2, right2)[n]
-            arrived(along2[p][n], block_kib)
-            targets = roles[p][:2] if s < 3 else (roles[p][3],) + roles[p][:2]
-            along1[p][s] = spread(p, i1, origin, a1, targets)
-            finished(p, i1, origin)
-
-    fwd1 = [[group() for _ in range(3)] for _ in range(2)]
-
-    def column(p, s):
-        right2, left2, _, opp2 = roles2[p]
-        return (axes[p][3], left2, right2, opp2)[s]
-
-    def pass_on(p, s):
-        right1, left1, _, _ = roles[p]
-        for side, origin in ((0, left1), (1, right1)):
-            arrived(along1[p][s][side], block_kib)
-            forward(p, origin, column(p, s), axes[p][0], roles[p][side], side, fwd1[p][s])
-            finished(p, origin, column(p, s))
-
-    for s in range(3):
+    for s in range(4):
         for p in range(2):
             pass_on(p, s)
-    for s in range(3):
+    for s in range(4):
         for p in range(2):
             arrived(fwd1[p][s], block_kib)
             finished(p, roles[p][3], column(p, s))
-    for n, role in ((1, 1), (2, 0), (0, 3)):
-        for p in range(2):
-            arrived(along1[p][3][n], block_kib)
-            finished(p, roles[p][role], column(p, 3))
     arrived(to_pair, size(o_w.at[0]))
     all_sent()
     assert groups[0] <= SEMS and groups[1] <= LOCAL_SEMS, (groups, sent)
@@ -454,11 +460,11 @@
             vmem((2, 2, V, WIDE), F32),
             vmem((2, V, WIDE), F32),
             vmem((2, 3, V, SUB), F32),
-            vmem((2, V, SUB), F32),
-            vmem((2, 7, TILE, SUB), F32),
+            vmem((2, 2, V, SUB // 2), F32),
+            vmem((2, 2, 7, TILE, SUB // 2), F32),
             vmem((2, TILE, SUB), F32),
-            vmem((16, 8, 128), F32),
-            vmem((16, 8, 128), F32),
+            vmem((16, 1, 128), F32),
+            vmem((16, 1, 128), F32),
             vmem((8, 2, 2, SUB), F32),
             vmem((8, 2, 2, SUB), BF16),
             vmem((8, 2, 2, SUB), BF16),
@@ -475,7 +481,7 @@
             vmem((2, 2, D), BF16),
             vmem((2, 2, 4), F32),
             vmem((2, 2, 4), F32),
-            vmem((LIMIT_KIB, 2, 128), F32),
+            vmem((2 * LIMIT_KIB, 1, 128), F32),
             pltpu.SemaphoreType.DMA((1,)),
             pltpu.SemaphoreType.DMA((SEMS,)),
             pltpu.SemaphoreType.DMA((LOCAL_SEMS,)),

time: 75.8 us -> 73.6 us (0.971)
  Pallas kernels: 75 us -> 72.9 us
    pallas_call x1, Pallas kernels: 72.9 us -> 70.7 us  [body(): pl.pallas_call(kernel, out_shape=(jax.ShapeDtypeStruct(master.shape, F32)...]
where the time goes in v5:
time: 73.6 us; the launch traced here: 73.5 us
  Pallas kernels  72.9 us (99%)
    pallas_call x1, Pallas kernels, body(): pl.pallas_call(kernel, out_shape=(jax.ShapeDtypeStruct(master.shape, F32)...  70.7 us
    pallas_call x1, Pallas kernels, body(): pl.pallas_call(write_out, out_shape=tuple((jax.ShapeDtypeStruct(a.shape,...  2.13 us

profile of v5, /device:TPU:1, one launch (start us, length us, event | category | flops | bytes accessed | tf_op | source)
XLA Modules:
  0.0 73.5 jit_solution(17836220144879516463)
XLA Ops:
  0.6 70.7 %step.1 = (f32[2,2,8192]{2,1,0:T(2,128)S(1)}, bf16[2,2,8192]{2,1,0:T(2,128)(2,1)S(1)}, bf16[2,2,8192]{2,1,0:T(2,128)(2,1)S(1)}, f32[2,2,4]{2,1,0:T(2,128)S(1)}, ...) custom-call(bf16[1,1,2,128,8192]{4,3,2,1,0:T(8,128)(2,1)} %part_in.1, f32[2,2,8192]{2,1,0:T(2,128)} %master_in.1, ...), custom_call_target="tpu_custom_call" | custom-call | tf_op jit(solution)/shard_map/step/pallas_call | solution.py:443
  71.4 2.1 %write_out.1 = (f32[2,2,8192]{2,1,0:T(2,128)}, bf16[2,2,8192]{2,1,0:T(2,128)(2,1)}, bf16[2,2,8192]{2,1,0:T(2,128)(2,1)}, f32[2,2,4]{2,1,0:T(2,128)}, f32[2,2,4]{2,1,0:T(2,128)}, /*index=5*/bf16[2,128,8192]{2,1,0:T(8,128)(2,1)}) custom-call(f32[2,2,8192]{2,1,0:T(2,128)S(1)} %get-tuple-element.12.refs_0_, bf16[2,2,8192]{2,1,0:T(2,128)(2,1)S(1)} %get-tuple-element.13.refs_1_, ...), custom_call_target="tpu_custom_call" | custom-call | tf_op jit(solution)/shard_map/write_out/pallas_call | solution.py:494

commit v6 on v5

--- a/solution.py
+++ b/solution.py
@@ -22,8 +22,9 @@
 SUB = 256
 NX, NY, NZ, NC = 4, 4, 8, 2
 TILE = 16
-SEMS = 80
-LOCAL_SEMS = 18
+SEMS = 81
+LOCAL_SEMS = 17
+DIRECT = (3,)
 LIMIT_KIB = 12 * 1024
 
 
@@ -38,8 +39,8 @@
 def adam(moment, second, scaled, master):
     m2 = 0.9 * moment + 0.1 * scaled
     v2 = 0.95 * second + 0.05 * scaled * scaled
-    update = m2 / (1.0 - 0.9**STEP) / (jnp.sqrt(v2 / (1.0 - 0.95**STEP)) + 1e-08)
-    return m2, v2, master - 0.01 * update
+    root = jnp.sqrt(v2 * (1.0 / (1.0 - 0.95**STEP))) + 1e-08
+    return m2, v2, master - m2 * (0.01 / (1.0 - 0.9**STEP)) / root
 
 
 def kernel(
@@ -344,6 +345,9 @@
             send(ref, ref, k, **{axis: target})
         return ks
 
+    def first_targets(p, s):
+        return roles[p][:2] + ((roles[p][3],) if s in DIRECT else ())
+
     def forward(p, i, j, axis, target, h, k):
         ref = o_w.at[c, rows_half[h], block_of(p, i, j)]
         send(ref, ref, k, **{axis: target})
@@ -363,7 +367,9 @@
 
         right2, left2, _, opp2 = roles2[p]
         along2[p] = spread(p, i1, i2, a2, (right2, left2, opp2))
-        along1[p][0] = spread(p, i1, i2, a1, roles[p][:2])
+    for p in range(2):
+        a1, i1, a2, i2 = axes[p]
+        along1[p][0] = spread(p, i1, i2, a1, first_targets(p, 0))
         finished(p, i1, i2)
 
     for n, s in ((1, 1), (0, 2), (2, 3)):
@@ -372,10 +378,10 @@
             right2, left2, _, opp2 = roles2[p]
             origin = (left2, right2, opp2)[n]
             arrived(along2[p][n], block_kib)
-            along1[p][s] = spread(p, i1, origin, a1, roles[p][:2])
+            along1[p][s] = spread(p, i1, origin, a1, first_targets(p, s))
             finished(p, i1, origin)
 
-    fwd1 = [[group() for _ in range(4)] for _ in range(2)]
+    fwd1 = [[None if s in DIRECT else group() for s in range(4)] for _ in range(2)]
 
     def column(p, s):
         right2, left2, _, opp2 = roles2[p]
@@ -385,7 +391,8 @@
         right1, left1, _, _ = roles[p]
         for side, origin in ((0, left1), (1, right1)):
             arrived(along1[p][s][side], block_kib)
-            forward(p, origin, column(p, s), axes[p][0], roles[p][side], side, fwd1[p][s])
+            if s not in DIRECT:
+                forward(p, origin, column(p, s), axes[p][0], roles[p][side], side, fwd1[p][s])
             finished(p, origin, column(p, s))
 
     arrived(q2, 3 * 32)
@@ -420,7 +427,7 @@
             pass_on(p, s)
     for s in range(4):
         for p in range(2):
-            arrived(fwd1[p][s], block_kib)
+            arrived(along1[p][s][2] if s in DIRECT else fwd1[p][s], block_kib)
             finished(p, roles[p][3], column(p, s))
     arrived(to_pair, size(o_w.at[0]))
     all_sent()

time: 73.6 us -> 72.6 us (0.986)
  Pallas kernels: 72.9 us -> 71.8 us
    pallas_call x1, Pallas kernels: 70.7 us -> 69.7 us  [body(): pl.pallas_call(kernel, out_shape=(jax.ShapeDtypeStruct(master.shape, F32)...]
where the time goes in v6:
time: 72.6 us; the launch traced here: 72.5 us
  Pallas kernels  71.8 us (99%)
    pallas_call x1, Pallas kernels, body(): pl.pallas_call(kernel, out_shape=(jax.ShapeDtypeStruct(master.shape, F32)...  69.7 us
    pallas_call x1, Pallas kernels, body(): pl.pallas_call(write_out, out_shape=tuple((jax.ShapeDtypeStruct(a.shape,...  2.13 us

profile of v6, /device:TPU:1, one launch (start us, length us, event | category | flops | bytes accessed | tf_op | source)
XLA Modules:
  0.0 72.5 jit_solution(7068232499810192797)
XLA Ops:
  0.6 69.7 %step.1 = (f32[2,2,8192]{2,1,0:T(2,128)S(1)}, bf16[2,2,8192]{2,1,0:T(2,128)(2,1)S(1)}, bf16[2,2,8192]{2,1,0:T(2,128)(2,1)S(1)}, f32[2,2,4]{2,1,0:T(2,128)S(1)}, ...) custom-call(bf16[1,1,2,128,8192]{4,3,2,1,0:T(8,128)(2,1)} %part_in.1, f32[2,2,8192]{2,1,0:T(2,128)} %master_in.1, ...), custom_call_target="tpu_custom_call" | custom-call | tf_op jit(solution)/shard_map/step/pallas_call | solution.py:450
  70.4 2.1 %write_out.1 = (f32[2,2,8192]{2,1,0:T(2,128)}, bf16[2,2,8192]{2,1,0:T(2,128)(2,1)}, bf16[2,2,8192]{2,1,0:T(2,128)(2,1)}, f32[2,2,4]{2,1,0:T(2,128)}, f32[2,2,4]{2,1,0:T(2,128)}, /*index=5*/bf16[2,128,8192]{2,1,0:T(8,128)(2,1)}) custom-call(f32[2,2,8192]{2,1,0:T(2,128)S(1)} %get-tuple-element.12.refs_0_, bf16[2,2,8192]{2,1,0:T(2,128)(2,1)S(1)} %get-tuple-element.13.refs_1_, ...), custom_call_target="tpu_custom_call" | custom-call | tf_op jit(solution)/shard_map/write_out/pallas_call | solution.py:501

commit v7 on v6

--- a/solution.py
+++ b/solution.py
@@ -22,7 +22,7 @@
 SUB = 256
 NX, NY, NZ, NC = 4, 4, 8, 2
 TILE = 16
-SEMS = 81
+SEMS = 73
 LOCAL_SEMS = 17
 DIRECT = (3,)
 LIMIT_KIB = 12 * 1024
@@ -159,7 +159,7 @@
     for k, dev in xc_peers:
         send(sc_stage.at[dev["c"]], e_s.at[own_k], state, **dev)
 
-    from_side = [[group() for _ in range(2)] for _ in range(2)]
+    from_side = [group() for _ in range(2)]
     for p in range(2):
         axis = axes[p][0]
         for side in range(2):
@@ -174,7 +174,7 @@
                 snd[p, side, rows, cc] = own[p, side, rows, cc].astype(F32) + par[p, side, rows, cc].astype(F32)
 
             cc = pl.ds(lo, WIDE // 2)
-            send(snd.at[p, side, :, cc], rcv2.at[p, side, :, cc], from_side[p][side], **{axis: roles[p][side]})
+            send(snd.at[p, side, :, cc], rcv2.at[p, side, :, cc], from_side[p], **{axis: roles[p][side]})
 
     for copy in own_state:
         copy.wait()
@@ -213,7 +213,7 @@
             tuple(2 * h + lax.rem(i2 + i2 // 2 + h + 1 - min(n, 1), 2) for h in range(2)) for n in range(3)
         ])
     starts, widths = (0, 0, SUB // 2), (SUB, SUB // 2, SUB // 2)
-    relay = [[[group() for _ in range(3)] for _ in range(2)] for _ in range(2)]
+    relay = [[group() for _ in range(3)] for _ in range(2)]
     for n in range(3):
         for p in range(2):
             axis = axes[p][0]
@@ -231,7 +231,7 @@
                     far = rcv1[p, side, 0, rows, cr].astype(F32) + rcv1[p, side, 1, rows, cr].astype(F32)
                     snd[p, side, rows, cc] = near + far
 
-                send(snd.at[p, side, :, cc], rcv2.at[p, side, :, cc], relay[p][side][n], **{axis: roles[p][side]})
+                send(snd.at[p, side, :, cc], rcv2.at[p, side, :, cc], relay[p][n], **{axis: roles[p][side]})
     pass_state(1)
 
     second = [[group() for _ in range(3)] for _ in range(2)]
@@ -241,10 +241,9 @@
             if n == 0:
                 own_loads[p][2].wait()
                 arrived(pair[p][2], size(par.at[p, 2]))
-                for side in range(2):
-                    arrived(from_side[p][side], size(rcv2.at[p, side]) // 2)
+                arrived(from_side[p], size(rcv2.at[p, 0]))
+            arrived(relay[p][n], 2 * V * widths[n] * 4 / 1024)
             for h in range(2):
-                arrived(relay[p][h][n], V * widths[n] * 4 / 1024)
                 cols = pl.ds(col(half_subs[p][n][h] * SUB + starts[n], SUB // 2), widths[n])
 
                 @pl.loop(0, V // TILE)

time: 72.6 us -> 72.5 us (level)
  no operation moved by 1% of the time
where the time goes in v7:
time: 72.5 us; the launch traced here: 72.4 us
  Pallas kernels  71.8 us (99%)
    pallas_call x1, Pallas kernels, body(): pl.pallas_call(kernel, out_shape=(jax.ShapeDtypeStruct(master.shape, F32)...  69.6 us
    pallas_call x1, Pallas kernels, body(): pl.pallas_call(write_out, out_shape=tuple((jax.ShapeDtypeStruct(a.shape,...  2.13 us

profile of v7, /device:TPU:1, one launch (start us, length us, event | category | flops | bytes accessed | tf_op | source)
XLA Modules:
  0.0 72.4 jit_solution(12144549563387860517)
XLA Ops:
  0.6 69.6 %step.1 = (f32[2,2,8192]{2,1,0:T(2,128)S(1)}, bf16[2,2,8192]{2,1,0:T(2,128)(2,1)S(1)}, bf16[2,2,8192]{2,1,0:T(2,128)(2,1)S(1)}, f32[2,2,4]{2,1,0:T(2,128)S(1)}, ...) custom-call(bf16[1,1,2,128,8192]{4,3,2,1,0:T(8,128)(2,1)} %part_in.1, f32[2,2,8192]{2,1,0:T(2,128)} %master_in.1, ...), custom_call_target="tpu_custom_call" | custom-call | tf_op jit(solution)/shard_map/step/pallas_call | solution.py:449
  70.3 2.1 %write_out.1 = (f32[2,2,8192]{2,1,0:T(2,128)}, bf16[2,2,8192]{2,1,0:T(2,128)(2,1)}, bf16[2,2,8192]{2,1,0:T(2,128)(2,1)}, f32[2,2,4]{2,1,0:T(2,128)}, f32[2,2,4]{2,1,0:T(2,128)}, /*index=5*/bf16[2,128,8192]{2,1,0:T(8,128)(2,1)}) custom-call(f32[2,2,8192]{2,1,0:T(2,128)S(1)} %get-tuple-element.12.refs_0_, bf16[2,2,8192]{2,1,0:T(2,128)(2,1)S(1)} %get-tuple-element.13.refs_1_, ...), custom_call_target="tpu_custom_call" | custom-call | tf_op jit(solution)/shard_map/write_out/pallas_call | solution.py:500
